TPU v7x, 8 devices: a whole 2x2x1 slice. The times are simulated.
8 devices in a mesh: dp: 1 (over z), ep: 2 (over y), sp: 4 (over x, core).
Axes of the slice: x: 2, y: 2, z: 1, core: 2. Of those that a mesh axis runs over, the one named last changes fastest.
Arguments:
- x_tokens: bfloat16 [2, 4096, 4096], P(('dp', 'ep'), 'sp')
- w_query: bfloat16 [4096, 4096], replicated
- w_key: bfloat16 [4096, 1024], replicated
- w_value: bfloat16 [4096, 1024], replicated
- w_out: bfloat16 [4096, 4096], replicated
- expert_ids: int32 [2, 4096, 2], P(('dp', 'ep'), 'sp')
- gate_probs: float32 [2, 4096, 16], P(('dp', 'ep'), 'sp')
Outputs:
- output 1: bfloat16 [2, 4096, 4096], P(('dp', 'ep'), 'sp')
- output 2: bfloat16 [4, 2, 16, 160, 4096], P(('dp', 'sp'), None, 'ep')
All inputs are finite; a program needn't handle non-finite values.
Results may differ from a plain program's by a relative error of at most 0.00895623.
Values are sent between devices in bfloat16 or wider.
A program may use at most 1 GiB of HBM per device.

v0:
```python
import math
import jax
import jax.numpy as jnp
from jax import lax
from jax.sharding import PartitionSpec as P

HEAD_DIM = 128


def capacity_of(tok_dev, top_k, experts):
    return max(8, 8 * ((5 * tok_dev * top_k + 32 * experts - 1) // (32 * experts)))


def attend(q_rows, k_all, v_all, q_offset):
    n_query, kv_count, group_size, head_dim = q_rows.shape
    seq_len = k_all.shape[0]
    q_block = n_query
    while q_block % 2 == 0 and q_block > 8 and q_block * kv_count * group_size * seq_len > 2 ** 24:
        q_block = q_block // 2
    n_blocks = n_query // q_block
    key_pos = jnp.arange(seq_len)
    inv_sqrt = 1.0 / math.sqrt(head_dim)

    def one_block(block_in):
        blk_index, q_blk = block_in
        scores = jnp.einsum('qkgd,skd->kgqs', q_blk, k_all, preferred_element_type=jnp.float32) * inv_sqrt
        query_pos = q_offset + blk_index * q_block + jnp.arange(q_block)
        scores = jnp.where(key_pos[None, :] <= query_pos[:, None], scores, -jnp.inf)
        prob_bf = jax.nn.softmax(scores, axis=-1).astype(jnp.bfloat16)
        block_out = jnp.einsum('kgqs,skd->qkgd', prob_bf, v_all, preferred_element_type=jnp.float32)
        return block_out.astype(jnp.bfloat16)

    block_outs = lax.map(one_block, (jnp.arange(n_blocks), q_rows.reshape(n_blocks, q_block, kv_count, group_size, head_dim)))
    return block_outs.reshape(n_query, kv_count, group_size, head_dim)


def dispatch_rows(hidden, ids_rows, gate_rows, capacity):
    tok_dev, d_model = hidden.shape
    top_k = ids_rows.shape[1]
    experts = gate_rows.shape[1]
    n_pairs = tok_dev * top_k
    gate_pick = jnp.take_along_axis(gate_rows, ids_rows, axis=1).reshape(n_pairs)
    flat_ids = ids_rows.reshape(n_pairs)
    one_hot = (flat_ids[:, None] == jnp.arange(experts)[None, :]).astype(jnp.int32)
    slot_rank = jnp.sum(jnp.cumsum(one_hot, axis=0) * one_hot, axis=1) - 1
    dest_row = jnp.where(slot_rank < capacity, flat_ids * capacity + slot_rank, experts * capacity)
    pair_tok = jnp.arange(n_pairs, dtype=jnp.int32) // top_k
    slot_tok = jnp.full((experts * capacity,), tok_dev, jnp.int32).at[dest_row].set(pair_tok, mode='drop')
    slot_gate = jnp.zeros((experts * capacity,), jnp.float32).at[dest_row].set(gate_pick, mode='drop')
    padded = jnp.concatenate([hidden, jnp.zeros((1, d_model), hidden.dtype)], axis=0)
    slot_rows = (jnp.take(padded, slot_tok, axis=0).astype(jnp.float32) * slot_gate[:, None]).astype(jnp.bfloat16)
    return slot_rows.reshape(experts, capacity, d_model)


def solution(mesh):
    ep_size = mesh.shape['ep']
    sp_size = mesh.shape['sp']

    def per_device(x_blk, w_query, w_key, w_value, w_out, ids_blk, gate_blk):
        x_rows = x_blk[0]
        tok_dev, d_model = x_rows.shape
        n_heads = w_query.shape[1] // HEAD_DIM
        kv_heads = w_key.shape[1] // HEAD_DIM
        experts = gate_blk.shape[2]
        capacity = capacity_of(tok_dev, ids_blk.shape[2], experts)
        kv_rep = max(1, sp_size // kv_heads)
        q_loc = jnp.dot(x_rows, w_query, preferred_element_type=jnp.float32).astype(jnp.bfloat16)
        k_loc = jnp.dot(x_rows, w_key, preferred_element_type=jnp.float32).astype(jnp.bfloat16)
        v_loc = jnp.dot(x_rows, w_value, preferred_element_type=jnp.float32).astype(jnp.bfloat16)
        if kv_rep > 1:
            k_loc = jnp.repeat(k_loc.reshape(tok_dev, kv_heads, HEAD_DIM), kv_rep, axis=1).reshape(tok_dev, kv_heads * kv_rep * HEAD_DIM)
            v_loc = jnp.repeat(v_loc.reshape(tok_dev, kv_heads, HEAD_DIM), kv_rep, axis=1).reshape(tok_dev, kv_heads * kv_rep * HEAD_DIM)
        q_seq = lax.all_to_all(q_loc, 'sp', 1, 0, tiled=True)
        k_seq = lax.all_to_all(k_loc, 'sp', 1, 0, tiled=True)
        v_seq = lax.all_to_all(v_loc, 'sp', 1, 0, tiled=True)
        seq_len = tok_dev * sp_size
        heads_loc = n_heads // sp_size
        kv_loc = kv_heads * kv_rep // sp_size
        attn_seq = attend(q_seq.reshape(seq_len, kv_loc, heads_loc // kv_loc, HEAD_DIM), k_seq.reshape(seq_len, kv_loc, HEAD_DIM), v_seq.reshape(seq_len, kv_loc, HEAD_DIM), 0)
        attn_rows = lax.all_to_all(attn_seq.reshape(seq_len, heads_loc * HEAD_DIM), 'sp', 0, 1, tiled=True)
        mixed = jnp.dot(attn_rows, w_out, preferred_element_type=jnp.float32)
        hidden = (x_rows.astype(jnp.float32) + mixed).astype(jnp.bfloat16)
        send_buf = dispatch_rows(hidden, ids_blk[0], gate_blk[0], capacity)
        received = lax.all_to_all(send_buf.reshape(ep_size, experts // ep_size, capacity, d_model), 'ep', 0, 0, tiled=True)
        return hidden[None], received[None]

    seq_spec = P(('dp', 'ep'), 'sp', None)
    buf_spec = P(('dp', 'sp'), None, 'ep', None, None)
    return jax.shard_map(per_device, mesh=mesh, in_specs=(seq_spec, P(), P(), P(), P(), seq_spec, seq_spec), out_specs=(seq_spec, buf_spec), check_vma=False)
```

profile of v0, /device:TPU:3, one launch (start us, length us, event | category | flops | bytes accessed | tf_op | source)
XLA Modules:
  0.0 1174.2 jit_solution(1986298489946756260)
XLA Ops:
  0.6 13.8 %fusion.38 = bf16[1024,1024]{0,1:T(8,128)(2,1)S(1)} fusion(bf16[4096,1024]{1,0:T(8,128)(2,1)} %param.11, bf16[1,1024,4096]{2,1,0:T(8,128)(2,1)} %param.9), kind=kOutput, calls=%fused_computation.40 | convolution fusion | flops 8590983168 | bytes 18874368 | tf_op jit(solution)/shard_map/dot_general | solution.py:68
  20.6 14.7 %fusion.41 = bf16[1024,1024]{0,1:T(8,128)(2,1)} fusion(bf16[4096,1024]{1,0:T(8,128)(2,1)} %param.12, bf16[1,1024,4096]{2,1,0:T(8,128)(2,1)} %param.9), kind=kOutput, calls=%fused_computation.41 | convolution fusion | flops 8590983168 | bytes 18874368 | tf_op jit(solution)/shard_map/dot_general | solution.py:69
  51.0 42.4 %fusion.35 = bf16[1024,4096]{1,0:T(8,128)(2,1)} fusion(bf16[4096,4096]{1,0:T(8,128)(2,1)} %param.10, bf16[1,1024,4096]{2,1,0:T(8,128)(2,1)} %param.9), kind=kOutput, calls=%fused_computation.39 | convolution fusion | flops 34363932672 | bytes 50331648 | tf_op jit(solution)/shard_map/dot_general | solution.py:67
  93.4 8.1 copy.41
  116.6 81.7 %all-to-all-done = bf16[1024,4,1024]{2,0,1:T(8,128)(2,1)} async-done(((bf16[1024,4,1024]{2,0,1:T(8,128)(2,1)}), bf16[1024,4,1024]{2,0,1:T(8,128)(2,1)}, u32[]{:S(2)}, u32[]{:S(2)}) %all-to-all-start) | async-done | bytes 8388640 | tf_op jit(solution)/shard_map/all_to_all | solution.py:73
  198.3 14.2 %reshape_reshape.2 = bf16[8,512,2,4,128]{4,3,2,1,0:T(4,128)(2,1)} reshape(bf16[4,1024,1024]{2,1,0:T(8,128)(2,1)} %bitcast.1) | data formatting | bytes 16777216 | tf_op jit(solution)/shard_map/reshape;reshape | solution.py:33
  212.5 493.8 %while.11 = (s32[]{:T(128)}, bf16[8,512,2,4,128]{4,3,2,1,0:T(4,128)(2,1)}, s32[8]{0:T(128)S(1)}, bf16[8,512,2,4,128]{4,3,2,1,0:T(4,128)(2,1)}, bf16[4096,2,128]{...) while((s32[]{:T(128)}, bf16[8,512,2,4,128]{4,3,2,1,0:T(4,128)(2,1)}, ...), condition=%wide.region_3.4_spmd.clone, body=%wide.region_0.3_spmd.clone.sunk | while | flops 8693223424 | bytes 148934784 | solution.py:33
  217.3 31.0 %fusion.73 = (f32[2,4,512]{2,1,0:T(4,128)S(1)}, f32[2,4,512,4096]{3,2,1,0:T(8,128)}) fusion(pred[512,4096]{1,0:T(8,128)(4,1)S(1)} %iota_compare_fusion.4, bf16[4096,2,128]{2,0,1:T(8,128)(2,1)} %get-tuple-element.135, bf16[1,512,2,4,128]{4,3,2,1,0:T(4,128)(2,1)S(1)} %constant_dynamic-slice_fusion.2), kind=kOutput, calls=%fused_computation.74.clone.1 | convolution fusion | flops 4362080256 | bytes 72368128 | tf_op jit(solution)/shard_map/while/body/eval_jaxpr/sub | solution.py:29
  248.3 24.2 %fusion.74 = bf16[1,512,2,4,128]{4,1,3,2,0:T(8,128)(2,1)S(1)} fusion(bf16[4096,2,128]{2,0,1:T(8,128)(2,1)} %get-tuple-element.136, f32[2,4,512,4096]{3,2,1,0:T(8,128)} %get-tuple-element.113, f32[2,4,512]{2,1,0:T(4,128)S(1)} %get-tuple-element.114), kind=kOutput, calls=%fused_computation.23.clone.1 | convolution fusion | flops 4329046016 | bytes 70270976 | tf_op jit(solution)/shard_map/while/body/eval_jaxpr/kgqs,skd->qkgd/dot_general | solution.py:30
  279.0 31.0 %fusion.73 = (f32[2,4,512]{2,1,0:T(4,128)S(1)}, f32[2,4,512,4096]{3,2,1,0:T(8,128)}) fusion(pred[512,4096]{1,0:T(8,128)(4,1)S(1)} %iota_compare_fusion.4, bf16[4096,2,128]{2,0,1:T(8,128)(2,1)} %get-tuple-element.135, bf16[1,512,2,4,128]{4,3,2,1,0:T(4,128)(2,1)S(1)} %constant_dynamic-slice_fusion.2), kind=kOutput, calls=%fused_computation.74.clone.1 | convolution fusion | flops 4362080256 | bytes 72368128 | tf_op jit(solution)/shard_map/while/body/eval_jaxpr/sub | solution.py:29
  310.0 24.2 %fusion.74 = bf16[1,512,2,4,128]{4,1,3,2,0:T(8,128)(2,1)S(1)} fusion(bf16[4096,2,128]{2,0,1:T(8,128)(2,1)} %get-tuple-element.136, f32[2,4,512,4096]{3,2,1,0:T(8,128)} %get-tuple-element.113, f32[2,4,512]{2,1,0:T(4,128)S(1)} %get-tuple-element.114), kind=kOutput, calls=%fused_computation.23.clone.1 | convolution fusion | flops 4329046016 | bytes 70270976 | tf_op jit(solution)/shard_map/while/body/eval_jaxpr/kgqs,skd->qkgd/dot_general | solution.py:30
  340.7 31.0 %fusion.73 = (f32[2,4,512]{2,1,0:T(4,128)S(1)}, f32[2,4,512,4096]{3,2,1,0:T(8,128)}) fusion(pred[512,4096]{1,0:T(8,128)(4,1)S(1)} %iota_compare_fusion.4, bf16[4096,2,128]{2,0,1:T(8,128)(2,1)} %get-tuple-element.135, bf16[1,512,2,4,128]{4,3,2,1,0:T(4,128)(2,1)S(1)} %constant_dynamic-slice_fusion.2), kind=kOutput, calls=%fused_computation.74.clone.1 | convolution fusion | flops 4362080256 | bytes 72368128 | tf_op jit(solution)/shard_map/while/body/eval_jaxpr/sub | solution.py:29
  371.7 24.2 %fusion.74 = bf16[1,512,2,4,128]{4,1,3,2,0:T(8,128)(2,1)S(1)} fusion(bf16[4096,2,128]{2,0,1:T(8,128)(2,1)} %get-tuple-element.136, f32[2,4,512,4096]{3,2,1,0:T(8,128)} %get-tuple-element.113, f32[2,4,512]{2,1,0:T(4,128)S(1)} %get-tuple-element.114), kind=kOutput, calls=%fused_computation.23.clone.1 | convolution fusion | flops 4329046016 | bytes 70270976 | tf_op jit(solution)/shard_map/while/body/eval_jaxpr/kgqs,skd->qkgd/dot_general | solution.py:30
  402.4 31.0 %fusion.73 = (f32[2,4,512]{2,1,0:T(4,128)S(1)}, f32[2,4,512,4096]{3,2,1,0:T(8,128)}) fusion(pred[512,4096]{1,0:T(8,128)(4,1)S(1)} %iota_compare_fusion.4, bf16[4096,2,128]{2,0,1:T(8,128)(2,1)} %get-tuple-element.135, bf16[1,512,2,4,128]{4,3,2,1,0:T(4,128)(2,1)S(1)} %constant_dynamic-slice_fusion.2), kind=kOutput, calls=%fused_computation.74.clone.1 | convolution fusion | flops 4362080256 | bytes 72368128 | tf_op jit(solution)/shard_map/while/body/eval_jaxpr/sub | solution.py:29
  433.4 24.2 %fusion.74 = bf16[1,512,2,4,128]{4,1,3,2,0:T(8,128)(2,1)S(1)} fusion(bf16[4096,2,128]{2,0,1:T(8,128)(2,1)} %get-tuple-element.136, f32[2,4,512,4096]{3,2,1,0:T(8,128)} %get-tuple-element.113, f32[2,4,512]{2,1,0:T(4,128)S(1)} %get-tuple-element.114), kind=kOutput, calls=%fused_computation.23.clone.1 | convolution fusion | flops 4329046016 | bytes 70270976 | tf_op jit(solution)/shard_map/while/body/eval_jaxpr/kgqs,skd->qkgd/dot_general | solution.py:30
  464.0 31.0 %fusion.73 = (f32[2,4,512]{2,1,0:T(4,128)S(1)}, f32[2,4,512,4096]{3,2,1,0:T(8,128)}) fusion(pred[512,4096]{1,0:T(8,128)(4,1)S(1)} %iota_compare_fusion.4, bf16[4096,2,128]{2,0,1:T(8,128)(2,1)} %get-tuple-element.135, bf16[1,512,2,4,128]{4,3,2,1,0:T(4,128)(2,1)S(1)} %constant_dynamic-slice_fusion.2), kind=kOutput, calls=%fused_computation.74.clone.1 | convolution fusion | flops 4362080256 | bytes 72368128 | tf_op jit(solution)/shard_map/while/body/eval_jaxpr/sub | solution.py:29
  495.0 24.2 %fusion.74 = bf16[1,512,2,4,128]{4,1,3,2,0:T(8,128)(2,1)S(1)} fusion(bf16[4096,2,128]{2,0,1:T(8,128)(2,1)} %get-tuple-element.136, f32[2,4,512,4096]{3,2,1,0:T(8,128)} %get-tuple-element.113, f32[2,4,512]{2,1,0:T(4,128)S(1)} %get-tuple-element.114), kind=kOutput, calls=%fused_computation.23.clone.1 | convolution fusion | flops 4329046016 | bytes 70270976 | tf_op jit(solution)/shard_map/while/body/eval_jaxpr/kgqs,skd->qkgd/dot_general | solution.py:30
  525.7 31.0 %fusion.73 = (f32[2,4,512]{2,1,0:T(4,128)S(1)}, f32[2,4,512,4096]{3,2,1,0:T(8,128)}) fusion(pred[512,4096]{1,0:T(8,128)(4,1)S(1)} %iota_compare_fusion.4, bf16[4096,2,128]{2,0,1:T(8,128)(2,1)} %get-tuple-element.135, bf16[1,512,2,4,128]{4,3,2,1,0:T(4,128)(2,1)S(1)} %constant_dynamic-slice_fusion.2), kind=kOutput, calls=%fused_computation.74.clone.1 | convolution fusion | flops 4362080256 | bytes 72368128 | tf_op jit(solution)/shard_map/while/body/eval_jaxpr/sub | solution.py:29
  556.7 24.2 %fusion.74 = bf16[1,512,2,4,128]{4,1,3,2,0:T(8,128)(2,1)S(1)} fusion(bf16[4096,2,128]{2,0,1:T(8,128)(2,1)} %get-tuple-element.136, f32[2,4,512,4096]{3,2,1,0:T(8,128)} %get-tuple-element.113, f32[2,4,512]{2,1,0:T(4,128)S(1)} %get-tuple-element.114), kind=kOutput, calls=%fused_computation.23.clone.1 | convolution fusion | flops 4329046016 | bytes 70270976 | tf_op jit(solution)/shard_map/while/body/eval_jaxpr/kgqs,skd->qkgd/dot_general | solution.py:30
  587.4 31.0 %fusion.73 = (f32[2,4,512]{2,1,0:T(4,128)S(1)}, f32[2,4,512,4096]{3,2,1,0:T(8,128)}) fusion(pred[512,4096]{1,0:T(8,128)(4,1)S(1)} %iota_compare_fusion.4, bf16[4096,2,128]{2,0,1:T(8,128)(2,1)} %get-tuple-element.135, bf16[1,512,2,4,128]{4,3,2,1,0:T(4,128)(2,1)S(1)} %constant_dynamic-slice_fusion.2), kind=kOutput, calls=%fused_computation.74.clone.1 | convolution fusion | flops 4362080256 | bytes 72368128 | tf_op jit(solution)/shard_map/while/body/eval_jaxpr/sub | solution.py:29
  618.4 24.2 %fusion.74 = bf16[1,512,2,4,128]{4,1,3,2,0:T(8,128)(2,1)S(1)} fusion(bf16[4096,2,128]{2,0,1:T(8,128)(2,1)} %get-tuple-element.136, f32[2,4,512,4096]{3,2,1,0:T(8,128)} %get-tuple-element.113, f32[2,4,512]{2,1,0:T(4,128)S(1)} %get-tuple-element.114), kind=kOutput, calls=%fused_computation.23.clone.1 | convolution fusion | flops 4329046016 | bytes 70270976 | tf_op jit(solution)/shard_map/while/body/eval_jaxpr/kgqs,skd->qkgd/dot_general | solution.py:30
  649.1 31.0 %fusion.73 = (f32[2,4,512]{2,1,0:T(4,128)S(1)}, f32[2,4,512,4096]{3,2,1,0:T(8,128)}) fusion(pred[512,4096]{1,0:T(8,128)(4,1)S(1)} %iota_compare_fusion.4, bf16[4096,2,128]{2,0,1:T(8,128)(2,1)} %get-tuple-element.135, bf16[1,512,2,4,128]{4,3,2,1,0:T(4,128)(2,1)S(1)} %constant_dynamic-slice_fusion.2), kind=kOutput, calls=%fused_computation.74.clone.1 | convolution fusion | flops 4362080256 | bytes 72368128 | tf_op jit(solution)/shard_map/while/body/eval_jaxpr/sub | solution.py:29
  680.1 24.2 %fusion.74 = bf16[1,512,2,4,128]{4,1,3,2,0:T(8,128)(2,1)S(1)} fusion(bf16[4096,2,128]{2,0,1:T(8,128)(2,1)} %get-tuple-element.136, f32[2,4,512,4096]{3,2,1,0:T(8,128)} %get-tuple-element.113, f32[2,4,512]{2,1,0:T(4,128)S(1)} %get-tuple-element.114), kind=kOutput, calls=%fused_computation.23.clone.1 | convolution fusion | flops 4329046016 | bytes 70270976 | tf_op jit(solution)/shard_map/while/body/eval_jaxpr/kgqs,skd->qkgd/dot_general | solution.py:30
  706.3 14.3 %all_to_all.62 = bf16[4,1024,1024]{2,1,0:T(8,128)(2,1)} reshape(bf16[8,512,2,4,128]{4,3,2,1,0:T(4,128)(2,1)} %get-tuple-element.39) | data formatting | bytes 16777216 | tf_op jit(solution)/shard_map/all_to_all | solution.py:80
  736.9 16.8 %gather_fusion.1 = f32[2048]{0:T(1024)S(1)} fusion(f32[1024,16]{0,1:T(8,128)S(1)} %bitcast.116, s32[2048]{0:T(1024)S(1)} %reshape.158), kind=kCustom, calls=%fused_computation.1 | custom fusion | bytes 32768 | tf_op jit(solution)/shard_map/jit(take_along_axis)/gather | solution.py:42
  754.0 8.1 scatter_custom_fusion.1
  770.3 48.9 %all-to-all-done.3 = bf16[4,1024,1024]{2,1,0:T(8,128)(2,1)} async-done(((bf16[4,1024,1024]{2,1,0:T(8,128)(2,1)}), bf16[4,1024,1024]{2,1,0:T(8,128)(2,1)}, u32[]{:S(2)}, u32[]{:S(2)}) %all-to-all-start.3) | async-done | bytes 8388640 | tf_op jit(solution)/shard_map/all_to_all | solution.py:80
  819.2 11.3 copy.16
  830.5 42.3 %add_convert_fusion = bf16[1024,4096]{1,0:T(8,128)(2,1)} fusion(bf16[1,1024,4096]{2,1,0:T(8,128)(2,1)} %param.9, bf16[1024,4096]{0,1:T(8,128)(2,1)} %bitcast.121, bf16[4096,4096]{1,0:T(8,128)(2,1)} %param.13), kind=kOutput, calls=%fused_computation.31 | convolution fusion | flops 34372321280 | bytes 58720256 | tf_op jit(solution)/shard_map/dot_general | solution.py:81
  880.6 40.0 %gather_fusion = bf16[2560,4096]{1,0:T(8,128)(2,1)} fusion(bf16[1025,4096]{1,0:T(8,128)(2,1)} %concatenate.3, s32[3072]{0:T(1024)S(1)} %pad_clamp_fusion), kind=kCustom, calls=%fused_computation | custom fusion | bytes 41953280 | tf_op jit(solution)/shard_map/jit(_take)/gather | solution.py:51
  920.6 13.9 %multiply_convert_fusion = bf16[2,8,160,4096]{3,2,1,0:T(8,128)(2,1)S(1)} fusion(f32[2,8,160]{2,1,0:T(8,128)S(1)} %mul.40, bf16[2,8,160,4096]{3,2,1,0:T(8,128)(2,1)} %bitcast.118, pred[2,8,160]{2,1,0:T(8,128)(4,1)S(1)} %broadcast_in_dim.62), kind=kLoop, calls=%fused_computation.30 | loop fusion | flops 41943040 | bytes 41955840 | tf_op jit(solution)/shard_map/convert_element_type | solution.py:51
  934.5 231.8 %all_to_all.72 = bf16[2,8,160,4096]{3,2,1,0:T(8,128)(2,1)S(1)} all-to-all(bf16[2,8,160,4096]{3,2,1,0:T(8,128)(2,1)S(1)} %multiply_convert_fusion), channel_id=1, replica_groups=mesh['dp'=1,'ep'=2,'sp'=4] {'ep'}, dimensions={0} | all-to-all | bytes 41943040 | tf_op jit(solution)/shard_map/all_to_all | solution.py:84
  (95 shorter events, 122.5 us)
Async XLA Ops:
  0.6 736.3 %copy-start = (f32[1,1024,16]{1,2,0:T(8,128)S(1)}, f32[1,1024,16]{1,2,0:T(8,128)}, u32[]{:S(2)}) copy-start(f32[1,1024,16]{1,2,0:T(8,128)} %param.15) | copy-start | bytes 196612
  17.0 27.2 %all-to-all-start.1 = ((bf16[1024,4,256]{2,0,1:T(8,128)(2,1)}), bf16[1024,4,256]{2,0,1:T(8,128)(2,1)S(1)}, u32[]{:S(2)}, u32[]{:S(2)}) async-start(bf16[1024,4,256]{2,0,1:T(8,128)(2,1)} %copy.10), calls=%async_computation.1 | async-start | bytes 4194304 | tf_op jit(solution)/shard_map/all_to_all | solution.py:74
  44.2 57.3 %all-to-all-start.2 = ((bf16[1024,4,256]{2,0,1:T(8,128)(2,1)}), bf16[1024,4,256]{2,0,1:T(8,128)(2,1)}, u32[]{:S(2)}, u32[]{:S(2)}) async-start(bf16[1024,4,256]{2,0,1:T(8,128)(2,1)} %copy.11), calls=%async_computation.2 | async-start | bytes 4194304 | tf_op jit(solution)/shard_map/all_to_all | solution.py:75
  101.5 96.8 %all-to-all-start = ((bf16[1024,4,1024]{2,0,1:T(8,128)(2,1)}), bf16[1024,4,1024]{2,0,1:T(8,128)(2,1)}, u32[]{:S(2)}, u32[]{:S(2)}) async-start(bf16[1024,4,1024]{2,0,1:T(8,128)(2,1)} %bitcast.119), calls=%async_computation | async-start | bytes 16777216 | tf_op jit(solution)/shard_map/all_to_all | solution.py:73
  720.6 7.5 copy-start.4
  720.6 98.6 %all-to-all-start.3 = ((bf16[4,1024,1024]{2,1,0:T(8,128)(2,1)}), bf16[4,1024,1024]{2,1,0:T(8,128)(2,1)}, u32[]{:S(2)}, u32[]{:S(2)}) async-start(bf16[4,1024,1024]{2,1,0:T(8,128)(2,1)} %all_to_all.62), calls=%async_computation.3 | async-start | bytes 16777216 | tf_op jit(solution)/shard_map/all_to_all | solution.py:80
  734.0 1.2 copy-start.1
  736.9 16.8 %copy-start.2 = (s32[16,16,128]{2,1,0:T(8,128)S(1)}, s32[16,16,128]{2,1,0:T(8,128)}, u32[]{:S(2)}) copy-start(s32[16,16,128]{2,1,0:T(8,128)} %copy-done.1) | copy-start | bytes 393220
  736.9 16.8 %copy-start.6 = (s32[16,17]{1,0:T(8,128)S(1)}, s32[16,17]{1,0:T(8,128)}, u32[]{:S(2)}) copy-start(s32[16,17]{1,0:T(8,128)} %reduce-window.9) | copy-start | bytes 3268
  736.9 16.9 %copy-start.3 = (s32[2048]{0:T(1024)S(1)}, s32[2048]{0:T(1024)}, u32[]{:S(2)}) copy-start(s32[2048]{0:T(1024)} %eq.25) | copy-start | bytes 24580
  736.9 17.0 %copy-start.5 = (s32[2048,1]{0,1:T(1,128)S(1)}, s32[2048,1]{0,1:T(1,128)}, u32[]{:S(2)}) copy-start(s32[2048,1]{0,1:T(1,128)} %mul.39) | copy-start | bytes 24580
where the time goes:
time: 1190 us; the launch traced here: 1170 us
  matrix products  555 us (47%)
  blocking collectives  232 us (19%)
  local copies, waits for them, and re-layouts  188 us (16%)
  waiting for transfers between devices  135 us (11%)
  other arithmetic  32.7 us (3%)
  starting transfers between devices  23.5 us (2%)
    sub x8, matrix products, one_block(): prob_bf = jax.nn.softmax(scores, axis=-1).astype(jnp.bfloat16)  248 us
    all_to_all x1, blocking collectives, per_device(): lax.all_to_all(send_buf.reshape(ep_size, experts // ep_size, capacity, d_...  232 us
    dot_general x8, matrix products, one_block(): jnp.einsum('kgqs,skd->qkgd', prob_bf, v_all, preferred_element_type=jnp.f...  194 us
    all_to_all x1, waiting for transfers between devices, per_device(): q_seq = lax.all_to_all(q_loc, 'sp', 1, 0, tiled=True)  81.7 us
    all_to_all x1, waiting for transfers between devices, per_device(): lax.all_to_all(attn_seq.reshape(seq_len, heads_loc * HEAD_DIM), 'sp', 0,...  48.9 us
    dot_general x1, matrix products, per_device(): jnp.dot(x_rows, w_query, preferred_element_type=jnp.float32)  42.4 us
    dot_general x1, matrix products, per_device(): mixed = jnp.dot(attn_rows, w_out, preferred_element_type=jnp.float32)  42.3 us
    gather x1, local copies, waits for them, and re-layouts, dispatch_rows(): jnp.take(padded, slot_tok, axis=0).astype(jnp.float32) * slot_gate[:, None]  40 us
  transfers between devices with their start and end apart: 4, of which 3 were waited for; matrix products, arithmetic and copies ran while one was open for 10% of the time, Pallas kernels for 0%

commit v1 on v0

v1 whole, which is shorter than its diff:
```python
import functools
import math
import jax
import jax.numpy as jnp
from jax import lax
from jax.experimental import pallas as pl
from jax.experimental.pallas import tpu as pltpu
from jax.sharding import PartitionSpec as P

HEAD_DIM = 128
KEY_BLOCK = 512
NEG = -0.7 * 3.4028235e38
BF16 = jnp.bfloat16
F32 = jnp.float32


def capacity_of(tok_dev, top_k, experts):
    return max(8, 8 * ((5 * tok_dev * top_k + 32 * experts - 1) // (32 * experts)))


def attend_kernel(group, diag_start, counts, q_ref, kd_ref, vd_ref, ko_ref, vo_ref, ka_ref, va_ref, kb_ref, vb_ref, o_ref, acc_ref):
    rows = q_ref.shape[0]
    scale = math.log2(math.e) / math.sqrt(HEAD_DIM)
    queries = [q_ref[:, h * HEAD_DIM:(h + 1) * HEAD_DIM] for h in range(group)]
    acc_ref[...] = jnp.zeros_like(acc_ref)

    def fold(k_blk, v_blk, state, mask):
        new_state = []
        for h in range(group):
            m_old, l_old = state[2 * h], state[2 * h + 1]
            s = lax.dot_general(k_blk, queries[h], (((1,), (1,)), ((), ())), preferred_element_type=F32)
            if mask is not None:
                s = jnp.where(mask, s, NEG)
            m_new = jnp.maximum(m_old, jnp.max(s, axis=0, keepdims=True))
            p = jnp.exp2(s * scale - m_new * scale)
            alpha = jnp.exp2((m_old - m_new) * scale)
            l_new = l_old * alpha + jnp.sum(p, axis=0, keepdims=True)
            pv = lax.dot_general(v_blk, p.astype(BF16), (((0,), (0,)), ((), ())), preferred_element_type=F32)
            acc_ref[h] = acc_ref[h] * alpha + pv
            new_state += [m_new, l_new]
        return tuple(new_state)

    def full(k_ref, v_ref, n_blocks, state):
        def step(i, st):
            start = pl.multiple_of(i * KEY_BLOCK, KEY_BLOCK)
            return fold(k_ref[pl.ds(start, KEY_BLOCK), :], v_ref[pl.ds(start, KEY_BLOCK), :], st, None)
        return lax.fori_loop(0, n_blocks, step, state)

    state = tuple(jnp.full((1, rows), NEG, F32) if i % 2 == 0 else jnp.zeros((1, rows), F32) for i in range(2 * group))
    per_block = ko_ref.shape[0] // KEY_BLOCK
    key_i = lax.broadcasted_iota(jnp.int32, (rows, rows), 0)
    qry_i = lax.broadcasted_iota(jnp.int32, (rows, rows), 1)
    state = fold(kd_ref[diag_start:diag_start + rows, :], vd_ref[diag_start:diag_start + rows, :], state, key_i <= qry_i)
    if diag_start:
        state = fold(kd_ref[:diag_start, :], vd_ref[:diag_start, :], state, None)
    state = full(ko_ref, vo_ref, counts[0] * per_block, state)
    state = full(ka_ref, va_ref, counts[1] * per_block, state)
    state = full(kb_ref, vb_ref, counts[1] * per_block, state)
    for h in range(group):
        o_t = acc_ref[h] * (1.0 / state[2 * h + 1])
        o_ref[:, h * HEAD_DIM:(h + 1) * HEAD_DIM] = o_t.T.astype(BF16)


def attend(counts, q_chunk, kvs, diag_start, kv_heads):
    rows, width = q_chunk.shape
    group = width // HEAD_DIM // kv_heads
    block = kvs[0].shape[0]
    kv_spec = pl.BlockSpec((block, HEAD_DIM), lambda g, c: (0, g))
    q_spec = pl.BlockSpec((rows, group * HEAD_DIM), lambda g, c: (0, g))
    return pl.pallas_call(
        functools.partial(attend_kernel, group, diag_start),
        grid_spec=pltpu.PrefetchScalarGridSpec(
            num_scalar_prefetch=1, grid=(kv_heads,), in_specs=[q_spec] + [kv_spec] * 8, out_specs=q_spec,
            scratch_shapes=[pltpu.VMEM((group, HEAD_DIM, rows), F32)]),
        out_shape=jax.ShapeDtypeStruct((rows, width), BF16),
        cost_estimate=pl.CostEstimate(flops=4 * rows * width * 3 * block, bytes_accessed=2 * (2 * rows * width + 8 * block * kv_heads * HEAD_DIM), transcendentals=rows * width // HEAD_DIM * 3 * block),
        compiler_params=pltpu.CompilerParams(dimension_semantics=('arbitrary',)),
        name='attend',
    )(counts, q_chunk, *kvs)


def build_kernel(capacity, n_parts, aliased, where, slot_ref, gate_ref, *refs):
    parts, (o_ref, pick_ref, scale_ref) = refs[:n_parts], refs[-3:]
    experts, tokens = slot_ref.shape

    @pl.when(pl.program_id(0) == 0)
    def _():
        rank = lax.broadcasted_iota(jnp.int32, (capacity, tokens), 0)
        for e in range(experts):
            hit = slot_ref[e:e + 1, :] == rank
            pick_ref[e * capacity:(e + 1) * capacity, :] = jnp.where(hit, 1.0, 0.0).astype(BF16)
            picked = jnp.sum(jnp.where(hit, gate_ref[e:e + 1, :], 0.0), axis=1, keepdims=True)
            scale_ref[e * capacity:(e + 1) * capacity, :] = jnp.broadcast_to(picked, (capacity, HEAD_DIM))

    for e in range(experts):
        lo, hi, at = e * capacity, (e + 1) * capacity, 0
        total = None
        for part in parts:
            n = part.shape[0]
            term = jnp.dot(pick_ref[lo:hi, at:at + n], part[...], preferred_element_type=F32)
            total = term if total is None else total + term
            at += n
        o_ref[0, 0, e] = (total * scale_ref[lo:hi, 0:1]).astype(BF16)


def build(where, slots, gates, parts, capacity, prior=None, col=512):
    experts, tokens = slots.shape
    d_model = parts[0].shape[1]
    fixed = pl.BlockSpec((experts, tokens), lambda n, w: (0, 0))
    in_specs = [fixed, fixed] + [pl.BlockSpec((p.shape[0], col), lambda n, w: (0, n)) for p in parts]
    args = [slots, gates, *parts]
    aliases = {}
    if prior is not None:
        in_specs.append(pl.BlockSpec(memory_space=pl.ANY))
        args.append(prior)
        aliases = {len(args): 0}
    return pl.pallas_call(
        functools.partial(build_kernel, capacity, len(parts), prior is not None),
        grid_spec=pltpu.PrefetchScalarGridSpec(
            num_scalar_prefetch=1, grid=(d_model // col,), in_specs=in_specs,
            out_specs=pl.BlockSpec((1, 1, experts, capacity, col), lambda n, w: (0, w[0], 0, 0, n)),
            scratch_shapes=[pltpu.VMEM((experts * capacity, tokens), BF16), pltpu.VMEM((experts * capacity, HEAD_DIM), F32)]),
        out_shape=jax.ShapeDtypeStruct((1, 2, experts, capacity, d_model), BF16),
        input_output_aliases=aliases,
        cost_estimate=pl.CostEstimate(flops=2 * experts * capacity * tokens * d_model, bytes_accessed=2 * d_model * (tokens + experts * capacity), transcendentals=0),
        compiler_params=pltpu.CompilerParams(dimension_semantics=('arbitrary',)),
        name='build',
    )(where, *args)


def slots_of(ids_rows, experts):
    tok_dev = ids_rows.shape[0]
    routed = jnp.any(ids_rows[:, :, None] == jnp.arange(experts)[None, None, :], axis=1)
    earlier = jnp.arange(tok_dev)[None, :] < jnp.arange(tok_dev)[:, None]
    rank = jnp.dot(earlier.astype(BF16), routed.astype(BF16), preferred_element_type=F32)
    return jnp.where(routed, rank, -1.0).astype(jnp.int32).T


def solution(mesh):
    sp_size = mesh.shape['sp']
    ep_size = mesh.shape['ep']
    pairs = [(i, i ^ 1) for i in range(sp_size)]
    across = [(0, 2), (1, 3)]
    ep_same = [(e * sp_size + s, (1 - e) * sp_size + s) for e in range(ep_size) for s in range(sp_size)]
    ep_cross = [(e * sp_size + s, (1 - e) * sp_size + (s ^ 1)) for e in range(ep_size) for s in range(sp_size)]

    def swap(a):
        return lax.ppermute(a, 'sp', pairs)

    def per_device(x_blk, w_query, w_key, w_value, w_out, ids_blk, gate_blk):
        x_own = x_blk[0]
        tok_dev, d_model = x_own.shape
        half = tok_dev // 2
        chunk = half // 2
        kv_heads = w_key.shape[1] // HEAD_DIM
        experts = gate_blk.shape[2]
        capacity = capacity_of(tok_dev, ids_blk.shape[2], experts)
        ep = lax.axis_index('ep')
        sp = lax.axis_index('sp')

        x_upper = swap(x_own[half:])
        k_own = jnp.dot(x_own, w_key, preferred_element_type=F32).astype(BF16)
        v_own = jnp.dot(x_own, w_value, preferred_element_type=F32).astype(BF16)
        k_a, v_a = lax.ppermute(k_own, 'sp', across), lax.ppermute(v_own, 'sp', across)
        k_mate, v_mate = swap(k_own), swap(v_own)
        k_b, v_b = swap(k_a), swap(v_a)
        q_low = jnp.dot(x_own[:half], w_query, preferred_element_type=F32).astype(BF16)
        q_upp = jnp.dot(x_upper, w_query, preferred_element_type=F32).astype(BF16)

        far = (sp >= 2).astype(jnp.int32)
        odd = (sp % 2).astype(jnp.int32)
        counts_low = jnp.stack([odd, far])
        counts_upp = jnp.stack([1 - odd, far])

        ids_other = lax.ppermute(ids_blk[0], ('ep', 'sp'), ep_same)
        gates_other = lax.ppermute(gate_blk[0], ('ep', 'sp'), ep_same)
        local = experts // ep_size

        def mine(a):
            return lax.dynamic_slice_in_dim(a, ep * local, local, 0)

        slots_own, gates_own = mine(slots_of(ids_blk[0], experts)), mine(gate_blk[0].T)
        slots_oth, gates_oth = mine(slots_of(ids_other, experts)), mine(gates_other.T)

        own_rows, other_rows = [], []
        for c in range(4):
            lower = c < 2
            at = (c % 2) * chunk
            q_c = lax.slice_in_dim(q_low if lower else q_upp, at, at + chunk, axis=0)
            x_c = lax.slice_in_dim(x_own if lower else x_upper, at, at + chunk, axis=0)
            diag = (k_own, v_own) if lower else (k_mate, v_mate)
            other = (k_mate, v_mate) if lower else (k_own, v_own)
            o_c = attend(counts_low if lower else counts_upp, q_c, (*diag, *other, k_a, v_a, k_b, v_b), c * chunk, kv_heads)
            mixed = jnp.dot(o_c, w_out, preferred_element_type=F32)
            h_c = (x_c.astype(F32) + mixed).astype(BF16)
            own_rows.append(h_c if lower else swap(h_c))
            other_rows.append(lax.ppermute(h_c, ('ep', 'sp'), ep_same if lower else ep_cross))
        hidden = jnp.concatenate(own_rows, axis=0)
        buf = build(ep[None].astype(jnp.int32), slots_own, gates_own, [hidden], capacity)
        buf = build((1 - ep)[None].astype(jnp.int32), slots_oth, gates_oth, other_rows, capacity, prior=buf)
        return hidden[None], buf

    seq_spec = P(('dp', 'ep'), 'sp', None)
    buf_spec = P(('dp', 'sp'), None, 'ep', None, None)
    return jax.shard_map(per_device, mesh=mesh, in_specs=(seq_spec, P(), P(), P(), P(), seq_spec, seq_spec), out_specs=(seq_spec, buf_spec), check_vma=False)
```

time: 1190 us -> 748 us (0.63)
  Pallas kernels: 0 us -> 442 us
  matrix products: 555 us -> 139 us
  blocking collectives: 232 us -> 0 us
  local copies, waits for them, and re-layouts: 188 us -> 13.3 us
  waiting for transfers between devices: 135 us -> 61 us
  starting transfers between devices: 23.5 us -> 73 us
  other arithmetic: 32.7 us -> 13.1 us
    pallas_call x0 -> x6, Pallas kernels: none -> 442 us  [the longest x4 410 us: attend(): pl.pallas_call(functools.partial(attend_kernel, group, diag_start), grid_...]
    sub x8 -> x0, matrix products: 248 us -> none  [one_block(): prob_bf = jax.nn.softmax(scores, axis=-1).astype(jnp.bfloat16)]
    all_to_all x1 -> x0, blocking collectives: 232 us -> none  [per_device(): lax.all_to_all(send_buf.reshape(ep_size, experts // ep_size, capacity, d_...]
    dot_general x12 -> x10, matrix products: 307 us -> 139 us  [the longest x4 68.9 us: per_device(): mixed = jnp.dot(o_c, w_out, preferred_element_type=F32)]
    all_to_all x4 -> x0, waiting for transfers between devices: 135 us -> none  [the longest x1 81.7 us: per_device(): q_seq = lax.all_to_all(q_loc, 'sp', 1, 0, tiled=True)]
    ppermute x0 -> x15, starting transfers between devices: none -> 73 us  [the longest x4 65.6 us: per_device(): lax.ppermute(h_c, ('ep', 'sp'), ep_same if lower else ep_cross)]
    ppermute x0 -> x15, waiting for transfers between devices: none -> 61 us  [the longest x1 43.7 us: per_device(): lax.ppermute(k_own, 'sp', across)]
    gather x4 -> x0, local copies, waits for them, and re-layouts: 57.3 us -> none  [the longest x1 40 us: dispatch_rows(): jnp.take(padded, slot_tok, axis=0).astype(jnp.float32) * slot_gate[:, None]]
  transfers between devices with their start and end apart: 4 -> 15, of which waited for: 3 -> 2; matrix products, arithmetic and copies ran while one was open for 10% -> 20% of each run, Pallas kernels for 0% -> 57%
where the time goes in v1:
time: 748 us; the launch traced here: 742 us
  Pallas kernels  442 us (59%)
  matrix products  139 us (19%)
  starting transfers between devices  73 us (10%)
  waiting for transfers between devices  61 us (8%)
  local copies, waits for them, and re-layouts  13.3 us (2%)
  other arithmetic  13.1 us (2%)
    pallas_call x4, Pallas kernels, attend(): pl.pallas_call(functools.partial(attend_kernel, group, diag_start), grid_...  410 us
    dot_general x4, matrix products, per_device(): mixed = jnp.dot(o_c, w_out, preferred_element_type=F32)  68.9 us
    ppermute x4, starting transfers between devices, per_device(): lax.ppermute(h_c, ('ep', 'sp'), ep_same if lower else ep_cross)  65.6 us
    ppermute x1, waiting for transfers between devices, per_device(): lax.ppermute(k_own, 'sp', across)  43.7 us
    pallas_call x2, Pallas kernels, build(): pl.pallas_call(functools.partial(build_kernel, capacity, len(parts), prio...  32.1 us
    dot_general x1, matrix products, per_device(): q_upp = jnp.dot(x_upper, w_query, preferred_element_type=F32).astype(BF16)  22.6 us
    dot_general x1, matrix products, per_device(): jnp.dot(x_own[:half], w_query, preferred_element_type=F32).astype(BF16)  22.4 us
    ppermute x4, waiting for transfers between devices, per_device(): lax.ppermute(h_c, ('ep', 'sp'), ep_same if lower else ep_cross)  17.3 us
  transfers between devices with their start and end apart: 15, of which 2 were waited for; matrix products, arithmetic and copies ran while one was open for 20% of the time, Pallas kernels for 57%

profile of v1, /device:TPU:3, one launch (start us, length us, event | category | flops | bytes accessed | tf_op | source)
XLA Modules:
  0.0 742.3 jit_solution(143438499533882178)
XLA Ops:
  0.7 13.8 %fusion.15.vd_ref.vo_ref = bf16[1024,1024]{1,0:T(8,128)(2,1)S(1)} fusion(bf16[4096,1024]{1,0:T(8,128)(2,1)} %param.10, bf16[1,1024,4096]{2,1,0:T(8,128)(2,1)} %param.7), kind=kOutput, calls=%fused_computation.22 | convolution fusion | flops 8590983168 | bytes 18874368 | tf_op jit(solution)/shard_map/dot_general | solution.py:163
  14.5 1.3 collective-permute-start.3
  15.8 0.7 collective-permute-start.1
  16.5 1.2 collective-permute-start.9
  17.7 10.1 %fusion.12.kd_ref.ko_ref = bf16[1024,1024]{1,0:T(8,128)(2,1)} fusion(bf16[4096,1024]{1,0:T(8,128)(2,1)S(1)} %copy-done.4, bf16[1,1024,4096]{2,1,0:T(8,128)(2,1)S(1)} %copy-done.1), kind=kOutput, calls=%fused_computation.21 | convolution fusion | flops 8590983168 | bytes 18874368 | tf_op jit(solution)/shard_map/dot_general | solution.py:162
  27.8 1.5 collective-permute-start.2
  29.3 2.3 slice_bitcast_fusion
  31.9 22.4 %convolution_convert_fusion.1 = bf16[512,4096]{1,0:T(8,128)(2,1)} fusion(bf16[4096,4096]{1,0:T(8,128)(2,1)} %param.8, bf16[1,1024,4096]{2,1,0:T(8,128)(2,1)S(1)} %copy-done.1), kind=kOutput, calls=%fused_computation.6 | convolution fusion | flops 17181966336 | bytes 41943040 | tf_op jit(solution)/shard_map/dot_general | solution.py:167
  54.8 1.4 dynamic-slice_bitcast_fusion.gate_ref
  57.3 4.7 fusion.25
  63.5 0.8 collective-permute-start.10
  64.2 43.7 %collective-permute-done.2.ka_ref = bf16[1024,1024]{1,0:T(8,128)(2,1)} collective-permute-done((bf16[1024,1024]{1,0:T(8,128)(2,1)}, bf16[1024,1024]{1,0:T(8,128)(2,1)}, u32[]{:S(2)}, u32[]{:S(2)}) %collective-permute-start.2) | collective-permute-done | bytes 2097184 | tf_op jit(solution)/shard_map/ppermute | solution.py:164
  108.0 1.4 collective-permute-start.5
  109.4 22.6 %convolution_convert_fusion = bf16[512,4096]{1,0:T(8,128)(2,1)S(1)} fusion(bf16[512,4096]{1,0:T(8,128)(2,1)} %collective-permute-done.6, bf16[4096,4096]{1,0:T(8,128)(2,1)} %param.8), kind=kOutput, calls=%fused_computation.5 | convolution fusion | flops 17181966336 | bytes 41943040 | tf_op jit(solution)/shard_map/dot_general | solution.py:168
  132.0 2.3 fusion.26
  134.3 90.7 %attend.6 = bf16[256,4096]{1,0:T(8,128)(2,1)} custom-call(s32[2]{0:T(128)} %pad_add_fusion.1.counts, bf16[256,4096]{1,0:T(8,128)(2,1)} %get-tuple-element.6.q_ref, bf16[1024,1024]{1,0:T(8,128)(2,1)} %collective-permute-done.ko_ref.kd_ref, bf16[1024,1024]{1,0:T(8,128)(2,1)} %collective-permute-done.1.vo_ref.vd_ref, bf16[1024,1024]{1,0:T(8,128)(2,1)} %fusion.12.kd_ref.ko_ref, ...), custom_call_target="tpu_custom_call" | custom-call | flops 12884901888 | bytes 20971520 | tf_op jit(solution)/shard_map/attend/pallas_call | solution.py:70
  225.0 17.2 %fusion.6 = bf16[256,4096]{1,0:T(8,128)(2,1)} fusion(bf16[256,4096]{1,0:T(8,128)(2,1)} %attend.6, bf16[4096,4096]{1,0:T(8,128)(2,1)} %param.11, bf16[512,4096]{1,0:T(8,128)(2,1)} %collective-permute-done.6), kind=kOutput, calls=%fused_computation.13 | convolution fusion | flops 8593080320 | bytes 39845888 | tf_op jit(solution)/shard_map/dot_general | solution.py:194
  242.2 32.5 %collective-permute-start.13 = (bf16[256,4096]{1,0:T(8,128)(2,1)}, bf16[256,4096]{1,0:T(8,128)(2,1)S(1)}, u32[]{:S(2)}, u32[]{:S(2)}) collective-permute-start(bf16[256,4096]{1,0:T(8,128)(2,1)} %fusion.6), channel_id=1, source_target_pairs={{0,5},{1,4},{2,7},{3,6},{4,1},{5,0},{6,3},{7,2}} | collective-permute-start | bytes 6291464 | tf_op jit(solution)/shard_map/ppermute | solution.py:197
  274.7 95.1 %attend.7 = bf16[256,4096]{1,0:T(8,128)(2,1)} custom-call(s32[2]{0:T(128)} %pad_add_fusion.1.counts, bf16[256,4096]{1,0:T(8,128)(2,1)} %get-tuple-element.7.q_ref, bf16[1024,1024]{1,0:T(8,128)(2,1)} %collective-permute-done.ko_ref.kd_ref, bf16[1024,1024]{1,0:T(8,128)(2,1)} %collective-permute-done.1.vo_ref.vd_ref, bf16[1024,1024]{1,0:T(8,128)(2,1)} %fusion.12.kd_ref.ko_ref, ...), custom_call_target="tpu_custom_call" | custom-call | flops 12884901888 | bytes 20971520 | tf_op jit(solution)/shard_map/attend/pallas_call | solution.py:70
  369.8 17.2 %fusion.7 = bf16[256,4096]{1,0:T(8,128)(2,1)} fusion(bf16[256,4096]{1,0:T(8,128)(2,1)} %attend.7, bf16[4096,4096]{1,0:T(8,128)(2,1)} %param.11, bf16[512,4096]{1,0:T(8,128)(2,1)} %collective-permute-done.6), kind=kOutput, calls=%fused_computation.14 | convolution fusion | flops 8593080320 | bytes 39845888 | tf_op jit(solution)/shard_map/dot_general | solution.py:194
  387.0 31.6 %collective-permute-start.14 = (bf16[256,4096]{1,0:T(8,128)(2,1)}, bf16[256,4096]{1,0:T(8,128)(2,1)}, u32[]{:S(2)}, u32[]{:S(2)}) collective-permute-start(bf16[256,4096]{1,0:T(8,128)(2,1)} %fusion.7), channel_id=1, source_target_pairs={{0,5},{1,4},{2,7},{3,6},{4,1},{5,0},{6,3},{7,2}} | collective-permute-start | bytes 6291464 | tf_op jit(solution)/shard_map/ppermute | solution.py:197
  418.6 117.0 %attend.5 = bf16[256,4096]{1,0:T(8,128)(2,1)} custom-call(s32[2]{0:T(128)} %pad_add_fusion.counts, bf16[256,4096]{1,0:T(8,128)(2,1)} %get-tuple-element.5.q_ref, bf16[1024,1024]{1,0:T(8,128)(2,1)} %fusion.12.kd_ref.ko_ref, bf16[1024,1024]{1,0:T(8,128)(2,1)} %copy-done.5, bf16[1024,1024]{1,0:T(8,128)(2,1)} %collective-permute-done.ko_ref.kd_ref, ...), custom_call_target="tpu_custom_call" | custom-call | flops 12884901888 | bytes 20971520 | tf_op jit(solution)/shard_map/attend/pallas_call | solution.py:70
  535.6 17.2 %fusion.5 = bf16[256,4096]{1,0:T(8,128)(2,1)} fusion(bf16[256,4096]{1,0:T(8,128)(2,1)} %attend.5, bf16[4096,4096]{1,0:T(8,128)(2,1)} %param.11, bf16[1,1024,4096]{2,1,0:T(8,128)(2,1)} %param.7), kind=kOutput, calls=%fused_computation.12 | convolution fusion | flops 8593080320 | bytes 39845888 | tf_op jit(solution)/shard_map/dot_general | solution.py:194
  552.8 107.4 %attend.4 = bf16[256,4096]{1,0:T(8,128)(2,1)} custom-call(s32[2]{0:T(128)} %pad_add_fusion.counts, bf16[256,4096]{1,0:T(8,128)(2,1)} %get-tuple-element.4.q_ref, bf16[1024,1024]{1,0:T(8,128)(2,1)} %fusion.12.kd_ref.ko_ref, bf16[1024,1024]{1,0:T(8,128)(2,1)} %copy-done.5, bf16[1024,1024]{1,0:T(8,128)(2,1)} %collective-permute-done.ko_ref.kd_ref, ...), custom_call_target="tpu_custom_call" | custom-call | flops 12884901888 | bytes 20971520 | tf_op jit(solution)/shard_map/attend/pallas_call | solution.py:70
  660.2 17.2 %fusion.4 = bf16[256,4096]{1,0:T(8,128)(2,1)} fusion(bf16[256,4096]{1,0:T(8,128)(2,1)} %attend.4, bf16[4096,4096]{1,0:T(8,128)(2,1)} %param.11, bf16[1,1024,4096]{2,1,0:T(8,128)(2,1)} %param.7), kind=kOutput, calls=%fused_computation.11 | convolution fusion | flops 8593080320 | bytes 39845888 | tf_op jit(solution)/shard_map/dot_general | solution.py:194
  677.4 1.2 collective-permute-start.11
  680.0 1.4 dynamic-slice_bitcast_fusion.1.gate_ref
  681.4 10.0 %pad_maximum_fusion = (bf16[1024,4096]{1,0:T(8,128)(2,1)}, bf16[1,1024,4096]{2,1,0:T(8,128)(2,1)}) fusion(bf16[256,4096]{1,0:T(8,128)(2,1)} %collective-permute-done.8, bf16[256,4096]{1,0:T(8,128)(2,1)} %collective-permute-done.7, bf16[256,4096]{1,0:T(8,128)(2,1)} %fusion.5, bf16[256,4096]{1,0:T(8,128)(2,1)} %fusion.4), kind=kLoop, calls=%fused_computation | loop fusion | flops 33554432 | bytes 25165824 | tf_op jit(solution)/shard_map/concatenate | solution.py:198
  691.4 16.1 %build.2.refs_4_ = bf16[1,2,8,160,4096]{4,3,2,1,0:T(8,128)(2,1)} custom-call(s32[1]{0:T(128)} %bitcast.14.where, s32[8,1024]{1,0:T(8,128)} %fusion.21.slot_ref, f32[8,1024]{1,0:T(8,128)} %dynamic-slice_bitcast_fusion.gate_ref, bf16[1024,4096]{1,0:T(8,128)(2,1)} %get-tuple-element.2.refs_0_), custom_call_target="tpu_custom_call" | custom-call | flops 10737418240 | bytes 18874368 | tf_op jit(solution)/shard_map/build/pallas_call | solution.py:117
  707.5 17.3 %collective-permute-done.12.refs_1_ = bf16[256,4096]{1,0:T(8,128)(2,1)} collective-permute-done((bf16[256,4096]{1,0:T(8,128)(2,1)}, bf16[256,4096]{1,0:T(8,128)(2,1)}, u32[]{:S(2)}, u32[]{:S(2)}) %collective-permute-start.12) | collective-permute-done | bytes 2097184 | tf_op jit(solution)/shard_map/ppermute | solution.py:197
  724.8 1.3 copy-done
  726.1 15.9 %build.3 = bf16[1,2,8,160,4096]{4,3,2,1,0:T(8,128)(2,1)} custom-call(s32[1]{0:T(128)} %bitcast.9.where, s32[8,1024]{1,0:T(8,128)} %fusion.23.slot_ref, f32[8,1024]{1,0:T(8,128)} %dynamic-slice_bitcast_fusion.1.gate_ref, bf16[256,4096]{1,0:T(8,128)(2,1)} %collective-permute-done.11.refs_0_, ...), custom_call_target="tpu_custom_call", output_to_operand_aliasing={{}: (7, {})} | custom-call | flops 10737418240 | bytes 18874368 | tf_op jit(solution)/shard_map/build/pallas_call | solution.py:117
  (38 shorter events, 4.9 us)
Async XLA Ops:
  0.6 17.1 %copy-start.1 = (bf16[1,1024,4096]{2,1,0:T(8,128)(2,1)S(1)}, bf16[1,1024,4096]{2,1,0:T(8,128)(2,1)}, u32[]{:S(2)}) copy-start(bf16[1,1024,4096]{2,1,0:T(8,128)(2,1)} %param.7) | copy-start | bytes 25165828
  0.6 15.8 %copy-start.3 = (s32[1,1024,2]{1,2,0:T(2,128)S(1)}, s32[1,1024,2]{1,2,0:T(2,128)}, u32[]{:S(2)}) copy-start(s32[1,1024,2]{1,2,0:T(2,128)} %param.12) | copy-start | bytes 24580
  0.7 17.1 %copy-start.4 = (bf16[4096,1024]{1,0:T(8,128)(2,1)S(1)}, bf16[4096,1024]{1,0:T(8,128)(2,1)}, u32[]{:S(2)}) copy-start(bf16[4096,1024]{1,0:T(8,128)(2,1)} %param.9) | copy-start | bytes 25165828
  14.5 13.3 %copy-start.5 = (bf16[1024,1024]{1,0:T(8,128)(2,1)}, bf16[1024,1024]{1,0:T(8,128)(2,1)S(1)}, u32[]{:S(2)}) copy-start(bf16[1024,1024]{1,0:T(8,128)(2,1)S(1)} %fusion.15.vd_ref.vo_ref) | copy-start | bytes 6291460
  14.5 49.0 %collective-permute-start.3 = (bf16[1024,1024]{1,0:T(8,128)(2,1)S(1)}, bf16[1024,1024]{1,0:T(8,128)(2,1)}, u32[]{:S(2)}, u32[]{:S(2)}) collective-permute-start(bf16[1024,1024]{1,0:T(8,128)(2,1)S(1)} %fusion.15.vd_ref.vo_ref), channel_id=1, source_target_pairs={{0,2},{1,3},{4,6},{5,7}} | collective-permute-start | bytes 6291464 | tf_op jit(solution)/shard_map/ppermute | solution.py:164
  15.8 118.5 %collective-permute-start.1 = (bf16[1024,1024]{1,0:T(8,128)(2,1)S(1)}, bf16[1024,1024]{1,0:T(8,128)(2,1)}, u32[]{:S(2)}, u32[]{:S(2)}) collective-permute-start(bf16[1024,1024]{1,0:T(8,128)(2,1)S(1)} %fusion.15.vd_ref.vo_ref), channel_id=1, source_target_pairs={{0,1},{1,0},{2,3},{3,2},{4,5},{5,4},{6,7},{7,6}} | collective-permute-start | bytes 6291464 | tf_op jit(solution)/shard_map/ppermute | solution.py:148
  16.5 46.2 %collective-permute-start.9 = (s32[1024,2]{0,1:T(2,128)S(1)}, s32[1024,2]{0,1:T(2,128)S(1)}, u32[]{:S(2)}, u32[]{:S(2)}) collective-permute-start(s32[1024,2]{0,1:T(2,128)S(1)} %bitcast.54), channel_id=1, source_target_pairs={{0,4},{1,5},{2,6},{3,7},{4,0},{5,1},{6,2},{7,3}} | collective-permute-start | bytes 24584 | tf_op jit(solution)/shard_map/ppermute | solution.py:175
  27.8 80.1 %collective-permute-start.2 = (bf16[1024,1024]{1,0:T(8,128)(2,1)}, bf16[1024,1024]{1,0:T(8,128)(2,1)}, u32[]{:S(2)}, u32[]{:S(2)}) collective-permute-start(bf16[1024,1024]{1,0:T(8,128)(2,1)} %fusion.12.kd_ref.ko_ref), channel_id=1, source_target_pairs={{0,2},{1,3},{4,6},{5,7}} | collective-permute-start | bytes 6291464 | tf_op jit(solution)/shard_map/ppermute | solution.py:164
  31.6 77.8 %collective-permute-start.6 = (bf16[512,4096]{1,0:T(8,128)(2,1)}, bf16[512,4096]{1,0:T(8,128)(2,1)}, u32[]{:S(2)}, u32[]{:S(2)}) collective-permute-start(bf16[512,4096]{1,0:T(8,128)(2,1)} %slice_bitcast_fusion), channel_id=1, source_target_pairs={{0,1},{1,0},{2,3},{3,2},{4,5},{5,4},{6,7},{7,6}} | collective-permute-start | bytes 12582920 | tf_op jit(solution)/shard_map/ppermute | solution.py:148
  62.6 71.7 %collective-permute-start = (bf16[1024,1024]{1,0:T(8,128)(2,1)}, bf16[1024,1024]{1,0:T(8,128)(2,1)}, u32[]{:S(2)}, u32[]{:S(2)}) collective-permute-start(bf16[1024,1024]{1,0:T(8,128)(2,1)} %fusion.12.kd_ref.ko_ref), channel_id=1, source_target_pairs={{0,1},{1,0},{2,3},{3,2},{4,5},{5,4},{6,7},{7,6}} | collective-permute-start | bytes 6291464 | tf_op jit(solution)/shard_map/ppermute | solution.py:148
  63.5 614.0 %collective-permute-start.10 = (f32[1024,16]{0,1:T(8,128)}, f32[1024,16]{0,1:T(8,128)}, u32[]{:S(2)}, u32[]{:S(2)}) collective-permute-start(f32[1024,16]{0,1:T(8,128)} %bitcast.12), channel_id=1, source_target_pairs={{0,4},{1,5},{2,6},{3,7},{4,0},{5,1},{6,2},{7,3}} | collective-permute-start | bytes 196616 | tf_op jit(solution)/shard_map/ppermute | solution.py:176
  108.0 26.3 %collective-permute-start.5 = (bf16[1024,1024]{1,0:T(8,128)(2,1)}, bf16[1024,1024]{1,0:T(8,128)(2,1)}, u32[]{:S(2)}, u32[]{:S(2)}) collective-permute-start(bf16[1024,1024]{1,0:T(8,128)(2,1)} %collective-permute-done.3.va_ref), channel_id=1, source_target_pairs={{0,1},{1,0},{2,3},{3,2},{4,5},{5,4},{6,7},{7,6}} | collective-permute-start | bytes 6291464 | tf_op jit(solution)/shard_map/ppermute | solution.py:148
  109.4 24.9 %collective-permute-start.4 = (bf16[1024,1024]{1,0:T(8,128)(2,1)}, bf16[1024,1024]{1,0:T(8,128)(2,1)}, u32[]{:S(2)}, u32[]{:S(2)}) collective-permute-start(bf16[1024,1024]{1,0:T(8,128)(2,1)} %collective-permute-done.2.ka_ref), channel_id=1, source_target_pairs={{0,1},{1,0},{2,3},{3,2},{4,5},{5,4},{6,7},{7,6}} | collective-permute-start | bytes 6291464 | tf_op jit(solution)/shard_map/ppermute | solution.py:148
  242.2 482.6 %collective-permute-start.13 = (bf16[256,4096]{1,0:T(8,128)(2,1)}, bf16[256,4096]{1,0:T(8,128)(2,1)S(1)}, u32[]{:S(2)}, u32[]{:S(2)}) collective-permute-start(bf16[256,4096]{1,0:T(8,128)(2,1)} %fusion.6), channel_id=1, source_target_pairs={{0,5},{1,4},{2,7},{3,6},{4,1},{5,0},{6,3},{7,2}} | collective-permute-start | bytes 6291464 | tf_op jit(solution)/shard_map/ppermute | solution.py:197
  274.7 403.9 %collective-permute-start.7 = (bf16[256,4096]{1,0:T(8,128)(2,1)}, bf16[256,4096]{1,0:T(8,128)(2,1)}, u32[]{:S(2)}, u32[]{:S(2)}) collective-permute-start(bf16[256,4096]{1,0:T(8,128)(2,1)} %fusion.6), channel_id=1, source_target_pairs={{0,1},{1,0},{2,3},{3,2},{4,5},{5,4},{6,7},{7,6}} | collective-permute-start | bytes 6291464 | tf_op jit(solution)/shard_map/ppermute | solution.py:148
  387.0 337.8 %collective-permute-start.14 = (bf16[256,4096]{1,0:T(8,128)(2,1)}, bf16[256,4096]{1,0:T(8,128)(2,1)}, u32[]{:S(2)}, u32[]{:S(2)}) collective-permute-start(bf16[256,4096]{1,0:T(8,128)(2,1)} %fusion.7), channel_id=1, source_target_pairs={{0,5},{1,4},{2,7},{3,6},{4,1},{5,0},{6,3},{7,2}} | collective-permute-start | bytes 6291464 | tf_op jit(solution)/shard_map/ppermute | solution.py:197
  418.6 262.8 %collective-permute-start.8 = (bf16[256,4096]{1,0:T(8,128)(2,1)}, bf16[256,4096]{1,0:T(8,128)(2,1)}, u32[]{:S(2)}, u32[]{:S(2)}) collective-permute-start(bf16[256,4096]{1,0:T(8,128)(2,1)} %fusion.7), channel_id=1, source_target_pairs={{0,1},{1,0},{2,3},{3,2},{4,5},{5,4},{6,7},{7,6}} | collective-permute-start | bytes 6291464 | tf_op jit(solution)/shard_map/ppermute | solution.py:148
  660.2 18.7 %copy-start.2 = (pred[1024,16]{0,1:T(8,128)(4,1)S(1)}, pred[1024,16]{0,1:T(8,128)(4,1)}, u32[]{:S(2)}) copy-start(pred[1024,16]{0,1:T(8,128)(4,1)} %fusion.18) | copy-start | bytes 49156
  677.4 30.1 %collective-permute-start.11 = (bf16[256,4096]{1,0:T(8,128)(2,1)}, bf16[256,4096]{1,0:T(8,128)(2,1)}, u32[]{:S(2)}, u32[]{:S(2)}) collective-permute-start(bf16[256,4096]{1,0:T(8,128)(2,1)} %fusion.4), channel_id=1, source_target_pairs={{0,4},{1,5},{2,6},{3,7},{4,0},{5,1},{6,2},{7,3}} | collective-permute-start | bytes 6291464 | tf_op jit(solution)/shard_map/ppermute | solution.py:197
  678.7 46.1 %collective-permute-start.12 = (bf16[256,4096]{1,0:T(8,128)(2,1)}, bf16[256,4096]{1,0:T(8,128)(2,1)}, u32[]{:S(2)}, u32[]{:S(2)}) collective-permute-start(bf16[256,4096]{1,0:T(8,128)(2,1)} %fusion.5), channel_id=1, source_target_pairs={{0,4},{1,5},{2,6},{3,7},{4,0},{5,1},{6,2},{7,3}} | collective-permute-start | bytes 6291464 | tf_op jit(solution)/shard_map/ppermute | solution.py:197
  724.8 1.3 copy-start

commit v2 on v1

--- a/solution.py
+++ b/solution.py
@@ -18,65 +18,120 @@
     return max(8, 8 * ((5 * tok_dev * top_k + 32 * experts - 1) // (32 * experts)))
 
 
-def attend_kernel(group, diag_start, counts, q_ref, kd_ref, vd_ref, ko_ref, vo_ref, ka_ref, va_ref, kb_ref, vb_ref, o_ref, acc_ref):
+def attend_kernel(group, diag_start, counts, q_ref, *refs):
+    (k_far0, v_far0, k_far1, v_far1, k_oth, v_oth, k_own, v_own, o_ref, k_buf, v_buf, s_ref, acc_ref, sems) = refs
+    g, n_g = pl.program_id(0), pl.num_programs(0)
     rows = q_ref.shape[0]
+    block = k_own.shape[0]
+    oth, far = counts[0], counts[1]
     scale = math.log2(math.e) / math.sqrt(HEAD_DIM)
-    queries = [q_ref[:, h * HEAD_DIM:(h + 1) * HEAD_DIM] for h in range(group)]
+    own_at = far * (2 * block) + oth * block
+    own_len = diag_start + rows
+    rest = own_len % KEY_BLOCK
+    last_len = rest if rest else KEY_BLOCK
+    n_full = (own_at + own_len - last_len) // KEY_BLOCK
+
+    def copies(head, slot):
+        def pair(k_src, v_src, at, n):
+            cols = pl.ds(head * HEAD_DIM, HEAD_DIM)
+            at = pl.multiple_of(at, 256)
+            return [pltpu.make_async_copy(k_src.at[pl.ds(0, n), cols], k_buf.at[slot, pl.ds(at, n), :], sems.at[slot, 0]),
+                    pltpu.make_async_copy(v_src.at[pl.ds(0, n), cols], v_buf.at[slot, pl.ds(at, n), :], sems.at[slot, 1])]
+        return (pair(k_far0, v_far0, 0, block) + pair(k_far1, v_far1, block, block),
+                pair(k_oth, v_oth, far * (2 * block), block), pair(k_own, v_own, own_at, own_len))
+
+    def each(head, slot, act):
+        far_c, oth_c, own_c = copies(head, slot)
+
+        @pl.when(far > 0)
+        def _():
+            for c in far_c:
+                act(c)
+
+        @pl.when(oth > 0)
+        def _():
+            for c in oth_c:
+                act(c)
+
+        for c in own_c:
+            act(c)
+
+    slot = lax.rem(g, 2)
+
+    @pl.when(g == 0)
+    def _():
+        each(0, 0, lambda c: c.start())
+
+    @pl.when(g + 1 < n_g)
+    def _():
+        each(g + 1, 1 - slot, lambda c: c.start())
+
+    each(g, slot, lambda c: c.wait())
     acc_ref[...] = jnp.zeros_like(acc_ref)
 
-    def fold(k_blk, v_blk, state, mask):
-        new_state = []
+    def score(i, h, n, masked):
+        k_blk = k_buf[slot, pl.ds(pl.multiple_of(i * KEY_BLOCK, KEY_BLOCK), n), :]
+        s = lax.dot_general(k_blk, q_ref[:, h * HEAD_DIM:(h + 1) * HEAD_DIM], (((1,), (1,)), ((), ())), preferred_element_type=F32)
+        if masked:
+            key_i = lax.broadcasted_iota(jnp.int32, (n, rows), 0)
+            qry_i = lax.broadcasted_iota(jnp.int32, (n, rows), 1) + (last_len - rows)
+            s = jnp.where(key_i <= qry_i, s, NEG)
+        s_ref[h % 2, :n, :] = s
+        return jnp.max(s, axis=0, keepdims=True)
+
+    def value(i, h, n, top, m_old, l_old):
+        m_new = jnp.maximum(m_old, top)
+        v_blk = v_buf[slot, pl.ds(pl.multiple_of(i * KEY_BLOCK, KEY_BLOCK), n), :]
+        p = jnp.exp2(s_ref[h % 2, :n, :] * scale - m_new * scale)
+        alpha = jnp.exp2((m_old - m_new) * scale)
+        l_new = l_old * alpha + jnp.sum(p, axis=0, keepdims=True)
+        pv = lax.dot_general(v_blk, p.astype(BF16), (((0,), (0,)), ((), ())), preferred_element_type=F32)
+        acc_ref[h] = acc_ref[h] * alpha + pv
+        return m_new, l_new
+
+    def step(i, carry):
+        top, ms, ls = carry
+        ms, ls = list(ms), list(ls)
         for h in range(group):
-            m_old, l_old = state[2 * h], state[2 * h + 1]
-            s = lax.dot_general(k_blk, queries[h], (((1,), (1,)), ((), ())), preferred_element_type=F32)
-            if mask is not None:
-                s = jnp.where(mask, s, NEG)
-            m_new = jnp.maximum(m_old, jnp.max(s, axis=0, keepdims=True))
-            p = jnp.exp2(s * scale - m_new * scale)
-            alpha = jnp.exp2((m_old - m_new) * scale)
-            l_new = l_old * alpha + jnp.sum(p, axis=0, keepdims=True)
-            pv = lax.dot_general(v_blk, p.astype(BF16), (((0,), (0,)), ((), ())), preferred_element_type=F32)
-            acc_ref[h] = acc_ref[h] * alpha + pv
-            new_state += [m_new, l_new]
-        return tuple(new_state)
-
-    def full(k_ref, v_ref, n_blocks, state):
-        def step(i, st):
-            start = pl.multiple_of(i * KEY_BLOCK, KEY_BLOCK)
-            return fold(k_ref[pl.ds(start, KEY_BLOCK), :], v_ref[pl.ds(start, KEY_BLOCK), :], st, None)
-        return lax.fori_loop(0, n_blocks, step, state)
-
-    state = tuple(jnp.full((1, rows), NEG, F32) if i % 2 == 0 else jnp.zeros((1, rows), F32) for i in range(2 * group))
-    per_block = ko_ref.shape[0] // KEY_BLOCK
-    key_i = lax.broadcasted_iota(jnp.int32, (rows, rows), 0)
-    qry_i = lax.broadcasted_iota(jnp.int32, (rows, rows), 1)
-    state = fold(kd_ref[diag_start:diag_start + rows, :], vd_ref[diag_start:diag_start + rows, :], state, key_i <= qry_i)
-    if diag_start:
-        state = fold(kd_ref[:diag_start, :], vd_ref[:diag_start, :], state, None)
-    state = full(ko_ref, vo_ref, counts[0] * per_block, state)
-    state = full(ka_ref, va_ref, counts[1] * per_block, state)
-    state = full(kb_ref, vb_ref, counts[1] * per_block, state)
+            if h + 1 < group:
+                top_next = score(i, h + 1, KEY_BLOCK, False)
+            else:
+                top_next = score(i + 1, 0, KEY_BLOCK, False)
+            ms[h], ls[h] = value(i, h, KEY_BLOCK, top, ms[h], ls[h])
+            top = top_next
+        return top, tuple(ms), tuple(ls)
+
+    m0 = tuple(jnp.full((1, rows), NEG, F32) for _ in range(group))
+    l0 = tuple(jnp.zeros((1, rows), F32) for _ in range(group))
+    top = lax.cond(n_full > 0, lambda: score(0, 0, KEY_BLOCK, False), lambda: jnp.zeros((1, rows), F32))
+    _, ms, ls = lax.fori_loop(0, n_full, step, (top, m0, l0))
+    top = score(n_full, 0, last_len, True)
     for h in range(group):
-        o_t = acc_ref[h] * (1.0 / state[2 * h + 1])
+        if h + 1 < group:
+            top_next = score(n_full, h + 1, last_len, True)
+        _, l_end = value(n_full, h, last_len, top, ms[h], ls[h])
+        top = top_next
+        o_t = acc_ref[h] * (1.0 / l_end)
         o_ref[:, h * HEAD_DIM:(h + 1) * HEAD_DIM] = o_t.T.astype(BF16)
 
 
-def attend(counts, q_chunk, kvs, diag_start, kv_heads):
+def attend(counts, q_chunk, own, other, far0, far1, diag_start, kv_heads):
     rows, width = q_chunk.shape
     group = width // HEAD_DIM // kv_heads
-    block = kvs[0].shape[0]
-    kv_spec = pl.BlockSpec((block, HEAD_DIM), lambda g, c: (0, g))
+    block = own[0].shape[0]
     q_spec = pl.BlockSpec((rows, group * HEAD_DIM), lambda g, c: (0, g))
     return pl.pallas_call(
         functools.partial(attend_kernel, group, diag_start),
         grid_spec=pltpu.PrefetchScalarGridSpec(
-            num_scalar_prefetch=1, grid=(kv_heads,), in_specs=[q_spec] + [kv_spec] * 8, out_specs=q_spec,
-            scratch_shapes=[pltpu.VMEM((group, HEAD_DIM, rows), F32)]),
+            num_scalar_prefetch=1, grid=(kv_heads,), in_specs=[q_spec] + [pl.BlockSpec(memory_space=pltpu.HBM)] * 8, out_specs=q_spec,
+            scratch_shapes=[pltpu.VMEM((2, 4 * block, HEAD_DIM), BF16), pltpu.VMEM((2, 4 * block, HEAD_DIM), BF16),
+                            pltpu.VMEM((2, KEY_BLOCK, rows), F32), pltpu.VMEM((group, HEAD_DIM, rows), F32),
+                            pltpu.SemaphoreType.DMA((2, 2))]),
         out_shape=jax.ShapeDtypeStruct((rows, width), BF16),
         cost_estimate=pl.CostEstimate(flops=4 * rows * width * 3 * block, bytes_accessed=2 * (2 * rows * width + 8 * block * kv_heads * HEAD_DIM), transcendentals=rows * width // HEAD_DIM * 3 * block),
         compiler_params=pltpu.CompilerParams(dimension_semantics=('arbitrary',)),
         name='attend',
-    )(counts, q_chunk, *kvs)
+    )(counts, q_chunk, *far0, *far1, *other, *own)
 
 
 def build_kernel(capacity, n_parts, aliased, where, slot_ref, gate_ref, *refs):
@@ -190,7 +245,7 @@
             x_c = lax.slice_in_dim(x_own if lower else x_upper, at, at + chunk, axis=0)
             diag = (k_own, v_own) if lower else (k_mate, v_mate)
             other = (k_mate, v_mate) if lower else (k_own, v_own)
-            o_c = attend(counts_low if lower else counts_upp, q_c, (*diag, *other, k_a, v_a, k_b, v_b), c * chunk, kv_heads)
+            o_c = attend(counts_low if lower else counts_upp, q_c, diag, other, (k_a, v_a), (k_b, v_b), c * chunk, kv_heads)
             mixed = jnp.dot(o_c, w_out, preferred_element_type=F32)
             h_c = (x_c.astype(F32) + mixed).astype(BF16)
             own_rows.append(h_c if lower else swap(h_c))

time: 748 us -> 552 us (0.74)
  Pallas kernels: 442 us -> 261 us
  starting transfers between devices: 73 us -> 42.6 us
  waiting for transfers between devices: 61 us -> 76.1 us
    pallas_call x4, Pallas kernels: 410 us -> 229 us  [attend(): pl.pallas_call(functools.partial(attend_kernel, group, diag_start), grid_...]
    ppermute x4, starting transfers between devices: 65.6 us -> 35.4 us  [per_device(): lax.ppermute(h_c, ('ep', 'sp'), ep_same if lower else ep_cross)]
    ppermute x4, waiting for transfers between devices: 17.3 us -> 31.5 us  [per_device(): lax.ppermute(h_c, ('ep', 'sp'), ep_same if lower else ep_cross)]
  transfers between devices with their start and end apart: 15 -> 15, of which waited for: 2 -> 4; matrix products, arithmetic and copies ran while one was open for 20% -> 28% of each run, Pallas kernels for 57% -> 45%
where the time goes in v2:
time: 552 us; the launch traced here: 546 us
  Pallas kernels  261 us (47%)
  matrix products  139 us (25%)
  waiting for transfers between devices  76.1 us (14%)
  starting transfers between devices  42.6 us (8%)
  local copies, waits for them, and re-layouts  13.3 us (2%)
  other arithmetic  13.1 us (2%)
    pallas_call x4, Pallas kernels, attend(): pl.pallas_call(functools.partial(attend_kernel, group, diag_start), grid_...  229 us
    dot_general x4, matrix products, per_device(): mixed = jnp.dot(o_c, w_out, preferred_element_type=F32)  69.4 us
    ppermute x1, waiting for transfers between devices, per_device(): lax.ppermute(k_own, 'sp', across)  43.7 us
    ppermute x4, starting transfers between devices, per_device(): lax.ppermute(h_c, ('ep', 'sp'), ep_same if lower else ep_cross)  35.4 us
    pallas_call x2, Pallas kernels, build(): pl.pallas_call(functools.partial(build_kernel, capacity, len(parts), prio...  32 us
    ppermute x4, waiting for transfers between devices, per_device(): lax.ppermute(h_c, ('ep', 'sp'), ep_same if lower else ep_cross)  31.5 us
    dot_general x1, matrix products, per_device(): q_upp = jnp.dot(x_upper, w_query, preferred_element_type=F32).astype(BF16)  22.6 us
    dot_general x1, matrix products, per_device(): jnp.dot(x_own[:half], w_query, preferred_element_type=F32).astype(BF16)  22.4 us
  transfers between devices with their start and end apart: 15, of which 4 were waited for; matrix products, arithmetic and copies ran while one was open for 28% of the time, Pallas kernels for 45%

profile of v2, /device:TPU:3, one launch (start us, length us, event | category | flops | bytes accessed | tf_op | source)
XLA Modules:
  0.0 546.3 jit_solution(14808167595684857208)
XLA Ops:
  0.7 13.8 %fusion.15.refs_7_.refs_5_ = bf16[1024,1024]{1,0:T(8,128)(2,1)S(1)} fusion(bf16[4096,1024]{1,0:T(8,128)(2,1)} %param.10, bf16[1,1024,4096]{2,1,0:T(8,128)(2,1)} %param.7), kind=kOutput, calls=%fused_computation.22 | convolution fusion | flops 8590983168 | bytes 18874368 | tf_op jit(solution)/shard_map/dot_general | solution.py:218
  15.2 1.3 collective-permute-start.1
  16.5 1.3 collective-permute-start.9
  17.7 10.1 %fusion.12.refs_6_.refs_4_ = bf16[1024,1024]{1,0:T(8,128)(2,1)} fusion(bf16[4096,1024]{1,0:T(8,128)(2,1)S(1)} %copy-done.4, bf16[1,1024,4096]{2,1,0:T(8,128)(2,1)S(1)} %copy-done.1), kind=kOutput, calls=%fused_computation.21 | convolution fusion | flops 8590983168 | bytes 18874368 | tf_op jit(solution)/shard_map/dot_general | solution.py:217
  27.8 1.5 collective-permute-start
  29.3 2.3 slice_bitcast_fusion
  31.9 22.4 %convolution_convert_fusion.1 = bf16[512,4096]{1,0:T(8,128)(2,1)} fusion(bf16[4096,4096]{1,0:T(8,128)(2,1)} %param.8, bf16[1,1024,4096]{2,1,0:T(8,128)(2,1)S(1)} %copy-done.1), kind=kOutput, calls=%fused_computation.6 | convolution fusion | flops 17181966336 | bytes 41943040 | tf_op jit(solution)/shard_map/dot_general | solution.py:222
  54.8 1.4 dynamic-slice_bitcast_fusion.gate_ref
  57.3 4.7 fusion.25
  63.5 0.9 collective-permute-done.1.refs_1_
  64.3 1.2 collective-permute-start.10
  65.6 43.7 %collective-permute-done.refs_0_ = bf16[1024,1024]{1,0:T(8,128)(2,1)} collective-permute-done((bf16[1024,1024]{1,0:T(8,128)(2,1)}, bf16[1024,1024]{1,0:T(8,128)(2,1)}, u32[]{:S(2)}, u32[]{:S(2)}) %collective-permute-start) | collective-permute-done | bytes 2097184 | tf_op jit(solution)/shard_map/ppermute | solution.py:219
  110.1 22.6 %convolution_convert_fusion = bf16[512,4096]{1,0:T(8,128)(2,1)S(1)} fusion(bf16[512,4096]{1,0:T(8,128)(2,1)} %collective-permute-done.6, bf16[4096,4096]{1,0:T(8,128)(2,1)} %param.8), kind=kOutput, calls=%fused_computation.5 | convolution fusion | flops 17181966336 | bytes 41943040 | tf_op jit(solution)/shard_map/dot_general | solution.py:223
  132.7 2.3 fusion.26
  135.0 52.1 %attend.6 = bf16[256,4096]{1,0:T(8,128)(2,1)} custom-call(s32[2]{0:T(128)} %pad_add_fusion.1.counts, bf16[256,4096]{1,0:T(8,128)(2,1)} %get-tuple-element.6.q_ref, bf16[1024,1024]{1,0:T(8,128)(2,1)} %collective-permute-done.refs_0_, bf16[1024,1024]{1,0:T(8,128)(2,1)} %collective-permute-done.1.refs_1_, bf16[1024,1024]{1,0:T(8,128)(2,1)} %collective-permute-done.2.refs_2_, ...), custom_call_target="tpu_custom_call" | custom-call | flops 12884901888 | bytes 20971520 | tf_op jit(solution)/shard_map/attend/pallas_call | solution.py:123
  187.1 17.4 %fusion.6 = bf16[256,4096]{1,0:T(8,128)(2,1)} fusion(bf16[256,4096]{1,0:T(8,128)(2,1)} %attend.6, bf16[4096,4096]{1,0:T(8,128)(2,1)} %param.11, bf16[512,4096]{1,0:T(8,128)(2,1)} %collective-permute-done.6), kind=kOutput, calls=%fused_computation.13 | convolution fusion | flops 8593080320 | bytes 39845888 | tf_op jit(solution)/shard_map/dot_general | solution.py:249
  204.6 17.4 %collective-permute-start.13 = (bf16[256,4096]{1,0:T(8,128)(2,1)}, bf16[256,4096]{1,0:T(8,128)(2,1)S(1)}, u32[]{:S(2)}, u32[]{:S(2)}) collective-permute-start(bf16[256,4096]{1,0:T(8,128)(2,1)} %fusion.6), channel_id=1, source_target_pairs={{0,5},{1,4},{2,7},{3,6},{4,1},{5,0},{6,3},{7,2}} | collective-permute-start | bytes 6291464 | tf_op jit(solution)/shard_map/ppermute | solution.py:252
  222.0 54.4 %attend.7 = bf16[256,4096]{1,0:T(8,128)(2,1)} custom-call(s32[2]{0:T(128)} %pad_add_fusion.1.counts, bf16[256,4096]{1,0:T(8,128)(2,1)} %get-tuple-element.7.q_ref, bf16[1024,1024]{1,0:T(8,128)(2,1)} %collective-permute-done.refs_0_, bf16[1024,1024]{1,0:T(8,128)(2,1)} %collective-permute-done.1.refs_1_, bf16[1024,1024]{1,0:T(8,128)(2,1)} %collective-permute-done.2.refs_2_, ...), custom_call_target="tpu_custom_call" | custom-call | flops 12884901888 | bytes 20971520 | tf_op jit(solution)/shard_map/attend/pallas_call | solution.py:123
  276.3 17.3 %fusion.7 = bf16[256,4096]{1,0:T(8,128)(2,1)} fusion(bf16[256,4096]{1,0:T(8,128)(2,1)} %attend.7, bf16[4096,4096]{1,0:T(8,128)(2,1)} %param.11, bf16[512,4096]{1,0:T(8,128)(2,1)} %collective-permute-done.6), kind=kOutput, calls=%fused_computation.14 | convolution fusion | flops 8593080320 | bytes 39845888 | tf_op jit(solution)/shard_map/dot_general | solution.py:249
  293.6 16.5 %collective-permute-start.14 = (bf16[256,4096]{1,0:T(8,128)(2,1)}, bf16[256,4096]{1,0:T(8,128)(2,1)}, u32[]{:S(2)}, u32[]{:S(2)}) collective-permute-start(bf16[256,4096]{1,0:T(8,128)(2,1)} %fusion.7), channel_id=1, source_target_pairs={{0,5},{1,4},{2,7},{3,6},{4,1},{5,0},{6,3},{7,2}} | collective-permute-start | bytes 6291464 | tf_op jit(solution)/shard_map/ppermute | solution.py:252
  310.1 62.3 %attend.5 = bf16[256,4096]{1,0:T(8,128)(2,1)} custom-call(s32[2]{0:T(128)} %pad_add_fusion.counts, bf16[256,4096]{1,0:T(8,128)(2,1)} %get-tuple-element.5.q_ref, bf16[1024,1024]{1,0:T(8,128)(2,1)} %collective-permute-done.refs_0_, bf16[1024,1024]{1,0:T(8,128)(2,1)} %collective-permute-done.1.refs_1_, bf16[1024,1024]{1,0:T(8,128)(2,1)} %collective-permute-done.2.refs_2_, ...), custom_call_target="tpu_custom_call" | custom-call | flops 12884901888 | bytes 20971520 | tf_op jit(solution)/shard_map/attend/pallas_call | solution.py:123
  372.4 17.5 %fusion.5 = bf16[256,4096]{1,0:T(8,128)(2,1)} fusion(bf16[256,4096]{1,0:T(8,128)(2,1)} %attend.5, bf16[4096,4096]{1,0:T(8,128)(2,1)} %param.11, bf16[1,1024,4096]{2,1,0:T(8,128)(2,1)} %param.7), kind=kOutput, calls=%fused_computation.12 | convolution fusion | flops 8593080320 | bytes 39845888 | tf_op jit(solution)/shard_map/dot_general | solution.py:249
  389.9 59.9 %attend.4 = bf16[256,4096]{1,0:T(8,128)(2,1)} custom-call(s32[2]{0:T(128)} %pad_add_fusion.counts, bf16[256,4096]{1,0:T(8,128)(2,1)} %get-tuple-element.4.q_ref, bf16[1024,1024]{1,0:T(8,128)(2,1)} %collective-permute-done.refs_0_, bf16[1024,1024]{1,0:T(8,128)(2,1)} %collective-permute-done.1.refs_1_, bf16[1024,1024]{1,0:T(8,128)(2,1)} %collective-permute-done.2.refs_2_, ...), custom_call_target="tpu_custom_call" | custom-call | flops 12884901888 | bytes 20971520 | tf_op jit(solution)/shard_map/attend/pallas_call | solution.py:123
  449.8 17.2 %fusion.4 = bf16[256,4096]{1,0:T(8,128)(2,1)} fusion(bf16[256,4096]{1,0:T(8,128)(2,1)} %attend.4, bf16[4096,4096]{1,0:T(8,128)(2,1)} %param.11, bf16[1,1024,4096]{2,1,0:T(8,128)(2,1)} %param.7), kind=kOutput, calls=%fused_computation.11 | convolution fusion | flops 8593080320 | bytes 39845888 | tf_op jit(solution)/shard_map/dot_general | solution.py:249
  467.1 1.2 collective-permute-start.11
  469.7 1.4 dynamic-slice_bitcast_fusion.1.gate_ref
  471.0 10.0 %pad_maximum_fusion = (bf16[1024,4096]{1,0:T(8,128)(2,1)}, bf16[1,1024,4096]{2,1,0:T(8,128)(2,1)}) fusion(bf16[256,4096]{1,0:T(8,128)(2,1)} %collective-permute-done.8, bf16[256,4096]{1,0:T(8,128)(2,1)} %collective-permute-done.7, bf16[256,4096]{1,0:T(8,128)(2,1)} %fusion.5, bf16[256,4096]{1,0:T(8,128)(2,1)} %fusion.4), kind=kLoop, calls=%fused_computation | loop fusion | flops 33554432 | bytes 25165824 | tf_op jit(solution)/shard_map/concatenate | solution.py:253
  481.0 16.1 %build.2.refs_4_ = bf16[1,2,8,160,4096]{4,3,2,1,0:T(8,128)(2,1)} custom-call(s32[1]{0:T(128)} %bitcast.14.where, s32[8,1024]{1,0:T(8,128)} %fusion.21.slot_ref, f32[8,1024]{1,0:T(8,128)} %dynamic-slice_bitcast_fusion.gate_ref, bf16[1024,4096]{1,0:T(8,128)(2,1)} %get-tuple-element.2.refs_0_), custom_call_target="tpu_custom_call" | custom-call | flops 10737418240 | bytes 18874368 | tf_op jit(solution)/shard_map/build/pallas_call | solution.py:172
  497.1 9.0 %collective-permute-done.11.refs_0_ = bf16[256,4096]{1,0:T(8,128)(2,1)} collective-permute-done((bf16[256,4096]{1,0:T(8,128)(2,1)}, bf16[256,4096]{1,0:T(8,128)(2,1)}, u32[]{:S(2)}, u32[]{:S(2)}) %collective-permute-start.11) | collective-permute-done | bytes 2097184 | tf_op jit(solution)/shard_map/ppermute | solution.py:252
  506.1 22.5 %collective-permute-done.12.refs_1_ = bf16[256,4096]{1,0:T(8,128)(2,1)} collective-permute-done((bf16[256,4096]{1,0:T(8,128)(2,1)}, bf16[256,4096]{1,0:T(8,128)(2,1)}, u32[]{:S(2)}, u32[]{:S(2)}) %collective-permute-start.12) | collective-permute-done | bytes 2097184 | tf_op jit(solution)/shard_map/ppermute | solution.py:252
  528.6 1.3 copy-done
  529.9 15.9 %build.3 = bf16[1,2,8,160,4096]{4,3,2,1,0:T(8,128)(2,1)} custom-call(s32[1]{0:T(128)} %bitcast.9.where, s32[8,1024]{1,0:T(8,128)} %fusion.23.slot_ref, f32[8,1024]{1,0:T(8,128)} %dynamic-slice_bitcast_fusion.1.gate_ref, bf16[256,4096]{1,0:T(8,128)(2,1)} %collective-permute-done.11.refs_0_, ...), custom_call_target="tpu_custom_call", output_to_operand_aliasing={{}: (7, {})} | custom-call | flops 10737418240 | bytes 18874368 | tf_op jit(solution)/shard_map/build/pallas_call | solution.py:172
  (38 shorter events, 6.3 us)
Async XLA Ops:
  0.6 17.1 %copy-start.1 = (bf16[1,1024,4096]{2,1,0:T(8,128)(2,1)S(1)}, bf16[1,1024,4096]{2,1,0:T(8,128)(2,1)}, u32[]{:S(2)}) copy-start(bf16[1,1024,4096]{2,1,0:T(8,128)(2,1)} %param.7) | copy-start | bytes 25165828
  0.6 15.8 %copy-start.3 = (s32[1,1024,2]{1,2,0:T(2,128)S(1)}, s32[1,1024,2]{1,2,0:T(2,128)}, u32[]{:S(2)}) copy-start(s32[1,1024,2]{1,2,0:T(2,128)} %param.12) | copy-start | bytes 24580
  0.7 17.1 %copy-start.4 = (bf16[4096,1024]{1,0:T(8,128)(2,1)S(1)}, bf16[4096,1024]{1,0:T(8,128)(2,1)}, u32[]{:S(2)}) copy-start(bf16[4096,1024]{1,0:T(8,128)(2,1)} %param.9) | copy-start | bytes 25165828
  14.5 13.3 %copy-start.5 = (bf16[1024,1024]{1,0:T(8,128)(2,1)}, bf16[1024,1024]{1,0:T(8,128)(2,1)S(1)}, u32[]{:S(2)}) copy-start(bf16[1024,1024]{1,0:T(8,128)(2,1)S(1)} %fusion.15.refs_7_.refs_5_) | copy-start | bytes 6291460
  14.5 120.5 %collective-permute-start.5 = (bf16[1024,1024]{1,0:T(8,128)(2,1)S(1)}, bf16[1024,1024]{1,0:T(8,128)(2,1)}, u32[]{:S(2)}, u32[]{:S(2)}) collective-permute-start(bf16[1024,1024]{1,0:T(8,128)(2,1)S(1)} %fusion.15.refs_7_.refs_5_), channel_id=1, source_target_pairs={{0,1},{1,0},{2,3},{3,2},{4,5},{5,4},{6,7},{7,6}} | collective-permute-start | bytes 6291464 | tf_op jit(solution)/shard_map/ppermute | solution.py:203
  15.2 49.2 %collective-permute-start.1 = (bf16[1024,1024]{1,0:T(8,128)(2,1)S(1)}, bf16[1024,1024]{1,0:T(8,128)(2,1)}, u32[]{:S(2)}, u32[]{:S(2)}) collective-permute-start(bf16[1024,1024]{1,0:T(8,128)(2,1)S(1)} %fusion.15.refs_7_.refs_5_), channel_id=1, source_target_pairs={{0,2},{1,3},{4,6},{5,7}} | collective-permute-start | bytes 6291464 | tf_op jit(solution)/shard_map/ppermute | solution.py:219
  16.5 46.2 %collective-permute-start.9 = (s32[1024,2]{0,1:T(2,128)S(1)}, s32[1024,2]{0,1:T(2,128)S(1)}, u32[]{:S(2)}, u32[]{:S(2)}) collective-permute-start(s32[1024,2]{0,1:T(2,128)S(1)} %bitcast.54), channel_id=1, source_target_pairs={{0,4},{1,5},{2,6},{3,7},{4,0},{5,1},{6,2},{7,3}} | collective-permute-start | bytes 24584 | tf_op jit(solution)/shard_map/ppermute | solution.py:230
  27.8 81.5 %collective-permute-start = (bf16[1024,1024]{1,0:T(8,128)(2,1)}, bf16[1024,1024]{1,0:T(8,128)(2,1)}, u32[]{:S(2)}, u32[]{:S(2)}) collective-permute-start(bf16[1024,1024]{1,0:T(8,128)(2,1)} %fusion.12.refs_6_.refs_4_), channel_id=1, source_target_pairs={{0,2},{1,3},{4,6},{5,7}} | collective-permute-start | bytes 6291464 | tf_op jit(solution)/shard_map/ppermute | solution.py:219
  31.6 78.5 %collective-permute-start.6 = (bf16[512,4096]{1,0:T(8,128)(2,1)}, bf16[512,4096]{1,0:T(8,128)(2,1)}, u32[]{:S(2)}, u32[]{:S(2)}) collective-permute-start(bf16[512,4096]{1,0:T(8,128)(2,1)} %slice_bitcast_fusion), channel_id=1, source_target_pairs={{0,1},{1,0},{2,3},{3,2},{4,5},{5,4},{6,7},{7,6}} | collective-permute-start | bytes 12582920 | tf_op jit(solution)/shard_map/ppermute | solution.py:203
  62.6 72.3 %collective-permute-start.4 = (bf16[1024,1024]{1,0:T(8,128)(2,1)}, bf16[1024,1024]{1,0:T(8,128)(2,1)}, u32[]{:S(2)}, u32[]{:S(2)}) collective-permute-start(bf16[1024,1024]{1,0:T(8,128)(2,1)} %fusion.12.refs_6_.refs_4_), channel_id=1, source_target_pairs={{0,1},{1,0},{2,3},{3,2},{4,5},{5,4},{6,7},{7,6}} | collective-permute-start | bytes 6291464 | tf_op jit(solution)/shard_map/ppermute | solution.py:203
  64.3 402.7 %collective-permute-start.10 = (f32[1024,16]{0,1:T(8,128)}, f32[1024,16]{0,1:T(8,128)}, u32[]{:S(2)}, u32[]{:S(2)}) collective-permute-start(f32[1024,16]{0,1:T(8,128)} %bitcast.12), channel_id=1, source_target_pairs={{0,4},{1,5},{2,6},{3,7},{4,0},{5,1},{6,2},{7,3}} | collective-permute-start | bytes 196616 | tf_op jit(solution)/shard_map/ppermute | solution.py:231
  109.3 25.7 %collective-permute-start.3 = (bf16[1024,1024]{1,0:T(8,128)(2,1)}, bf16[1024,1024]{1,0:T(8,128)(2,1)}, u32[]{:S(2)}, u32[]{:S(2)}) collective-permute-start(bf16[1024,1024]{1,0:T(8,128)(2,1)} %collective-permute-done.1.refs_1_), channel_id=1, source_target_pairs={{0,1},{1,0},{2,3},{3,2},{4,5},{5,4},{6,7},{7,6}} | collective-permute-start | bytes 6291464 | tf_op jit(solution)/shard_map/ppermute | solution.py:203
  110.1 24.9 %collective-permute-start.2 = (bf16[1024,1024]{1,0:T(8,128)(2,1)}, bf16[1024,1024]{1,0:T(8,128)(2,1)}, u32[]{:S(2)}, u32[]{:S(2)}) collective-permute-start(bf16[1024,1024]{1,0:T(8,128)(2,1)} %collective-permute-done.refs_0_), channel_id=1, source_target_pairs={{0,1},{1,0},{2,3},{3,2},{4,5},{5,4},{6,7},{7,6}} | collective-permute-start | bytes 6291464 | tf_op jit(solution)/shard_map/ppermute | solution.py:203
  204.6 324.1 %collective-permute-start.13 = (bf16[256,4096]{1,0:T(8,128)(2,1)}, bf16[256,4096]{1,0:T(8,128)(2,1)S(1)}, u32[]{:S(2)}, u32[]{:S(2)}) collective-permute-start(bf16[256,4096]{1,0:T(8,128)(2,1)} %fusion.6), channel_id=1, source_target_pairs={{0,5},{1,4},{2,7},{3,6},{4,1},{5,0},{6,3},{7,2}} | collective-permute-start | bytes 6291464 | tf_op jit(solution)/shard_map/ppermute | solution.py:252
  222.0 246.3 %collective-permute-start.7 = (bf16[256,4096]{1,0:T(8,128)(2,1)}, bf16[256,4096]{1,0:T(8,128)(2,1)}, u32[]{:S(2)}, u32[]{:S(2)}) collective-permute-start(bf16[256,4096]{1,0:T(8,128)(2,1)} %fusion.6), channel_id=1, source_target_pairs={{0,1},{1,0},{2,3},{3,2},{4,5},{5,4},{6,7},{7,6}} | collective-permute-start | bytes 6291464 | tf_op jit(solution)/shard_map/ppermute | solution.py:203
  293.6 235.0 %collective-permute-start.14 = (bf16[256,4096]{1,0:T(8,128)(2,1)}, bf16[256,4096]{1,0:T(8,128)(2,1)}, u32[]{:S(2)}, u32[]{:S(2)}) collective-permute-start(bf16[256,4096]{1,0:T(8,128)(2,1)} %fusion.7), channel_id=1, source_target_pairs={{0,5},{1,4},{2,7},{3,6},{4,1},{5,0},{6,3},{7,2}} | collective-permute-start | bytes 6291464 | tf_op jit(solution)/shard_map/ppermute | solution.py:252
  310.1 160.9 %collective-permute-start.8 = (bf16[256,4096]{1,0:T(8,128)(2,1)}, bf16[256,4096]{1,0:T(8,128)(2,1)}, u32[]{:S(2)}, u32[]{:S(2)}) collective-permute-start(bf16[256,4096]{1,0:T(8,128)(2,1)} %fusion.7), channel_id=1, source_target_pairs={{0,1},{1,0},{2,3},{3,2},{4,5},{5,4},{6,7},{7,6}} | collective-permute-start | bytes 6291464 | tf_op jit(solution)/shard_map/ppermute | solution.py:203
  449.8 18.7 %copy-start.2 = (pred[1024,16]{0,1:T(8,128)(4,1)S(1)}, pred[1024,16]{0,1:T(8,128)(4,1)}, u32[]{:S(2)}) copy-start(pred[1024,16]{0,1:T(8,128)(4,1)} %fusion.18) | copy-start | bytes 49156
  467.1 39.0 %collective-permute-start.11 = (bf16[256,4096]{1,0:T(8,128)(2,1)}, bf16[256,4096]{1,0:T(8,128)(2,1)}, u32[]{:S(2)}, u32[]{:S(2)}) collective-permute-start(bf16[256,4096]{1,0:T(8,128)(2,1)} %fusion.4), channel_id=1, source_target_pairs={{0,4},{1,5},{2,6},{3,7},{4,0},{5,1},{6,2},{7,3}} | collective-permute-start | bytes 6291464 | tf_op jit(solution)/shard_map/ppermute | solution.py:252
  468.3 60.3 %collective-permute-start.12 = (bf16[256,4096]{1,0:T(8,128)(2,1)}, bf16[256,4096]{1,0:T(8,128)(2,1)}, u32[]{:S(2)}, u32[]{:S(2)}) collective-permute-start(bf16[256,4096]{1,0:T(8,128)(2,1)} %fusion.5), channel_id=1, source_target_pairs={{0,4},{1,5},{2,6},{3,7},{4,0},{5,1},{6,2},{7,3}} | collective-permute-start | bytes 6291464 | tf_op jit(solution)/shard_map/ppermute | solution.py:252
  528.6 1.3 copy-start

commit v3 on v1

v3 whole, which is shorter than its diff:
```python
import functools
import math
import jax
import jax.numpy as jnp
from jax import lax
from jax.experimental import pallas as pl
from jax.experimental.pallas import tpu as pltpu
from jax.sharding import PartitionSpec as P

HEAD_DIM = 128
TILE = 256
NEG = -0.7 * 3.4028235e38
BF16 = jnp.bfloat16
F32 = jnp.float32


def capacity_of(tok_dev, top_k, experts):
    return max(8, 8 * ((5 * tok_dev * top_k + 32 * experts - 1) // (32 * experts)))


def fold_blocks(items, q_ref, s_ref, acc_ref, m_l):
    rows = q_ref.shape[0]
    scale = math.log2(math.e) / math.sqrt(HEAD_DIM)

    def score(idx, at):
        h, k_ref, _, start, _, masked = items[idx]
        s = lax.dot_general(k_ref[start + at:start + at + TILE, :], q_ref[:, h * HEAD_DIM:(h + 1) * HEAD_DIM], (((1,), (1,)), ((), ())), preferred_element_type=F32)
        if masked is not None and at + TILE > masked:
            key_i = lax.broadcasted_iota(jnp.int32, (TILE, rows), 0) + (at - masked)
            qry_i = lax.broadcasted_iota(jnp.int32, (TILE, rows), 1)
            s = jnp.where(key_i <= qry_i, s, NEG)
        s_ref[idx % 2, at:at + TILE, :] = s
        return jnp.max(s, axis=0, keepdims=True)

    def join(top, t):
        return t if top is None else jnp.maximum(top, t)

    top = None
    for at in range(0, items[0][4], TILE):
        top = join(top, score(0, at))
    for idx, (h, _, v_ref, start, n, _) in enumerate(items):
        n_next = items[idx + 1][4] if idx + 1 < len(items) else 0
        m_old, l_old = m_l[h]
        m_new = jnp.maximum(m_old, top)
        shift = m_new * scale
        alpha = jnp.exp2((m_old - m_new) * scale)
        l_new = l_old * alpha
        top, pv = None, None
        for at in range(0, max(n, n_next), TILE):
            if at < n_next:
                top = join(top, score(idx + 1, at))
            if at < n:
                p = jnp.exp2(s_ref[idx % 2, at:at + TILE, :] * scale - shift)
                l_new = l_new + jnp.sum(p, axis=0, keepdims=True)
                term = lax.dot_general(v_ref[start + at:start + at + TILE, :], p.astype(BF16), (((0,), (0,)), ((), ())), preferred_element_type=F32)
                pv = term if pv is None else pv + term
        acc_ref[h] = acc_ref[h] * alpha + pv
        m_l[h] = (m_new, l_new)
    return m_l


def near_kernel(group, diag_start, counts, q_ref, k_oth, v_oth, k_own, v_own, acc_ref, ml_ref, s_ref):
    rows = q_ref.shape[0]
    acc = acc_ref.at[0]
    acc[...] = jnp.zeros_like(acc)
    ml_ref[0, :group] = jnp.full((group, rows), NEG, F32)
    ml_ref[0, group:] = jnp.zeros((group, rows), F32)

    def run(items):
        m_l = [(ml_ref[0, h:h + 1], ml_ref[0, group + h:group + h + 1]) for h in range(group)]
        for h, (m, l) in enumerate(fold_blocks(items, q_ref, s_ref, acc, m_l)):
            ml_ref[0, h:h + 1] = m
            ml_ref[0, group + h:group + h + 1] = l

    @pl.when(counts[0] > 0)
    def _():
        run([(h, k_oth, v_oth, 0, k_oth.shape[0], None) for h in range(group)])

    run([(h, k_own, v_own, 0, diag_start + rows, diag_start) for h in range(group)])


def far_kernel(group, counts, q_ref, acc_in, ml_ref, ka, va, kb, vb, *refs):
    o_ref, s_ref, acc_ref = refs[-3:]
    acc_ref[...] = acc_in[0]

    def put(m_l):
        for h, (_, l) in enumerate(m_l):
            o_t = acc_ref[h] * (1.0 / l)
            o_ref[:, h * HEAD_DIM:(h + 1) * HEAD_DIM] = o_t.T.astype(BF16)

    m_l = [(ml_ref[0, h:h + 1], ml_ref[0, group + h:group + h + 1]) for h in range(group)]

    @pl.when(counts[1] > 0)
    def _():
        n = ka.shape[0]
        put(fold_blocks([(h, k, v, 0, n, None) for k, v in ((ka, va), (kb, vb)) for h in range(group)], q_ref, s_ref, acc_ref, list(m_l)))

    @pl.when(counts[1] == 0)
    def _():
        put(m_l)


def attend_near(counts, q, part, own, other, diag_start, kv_heads, rows):
    width = q.shape[1]
    group = width // HEAD_DIM // kv_heads
    block = own[0].shape[0]
    q_spec = pl.BlockSpec((rows, group * HEAD_DIM), lambda g, c: (part, g))
    kv_spec = pl.BlockSpec((block, HEAD_DIM), lambda g, c: (0, g))
    return pl.pallas_call(
        functools.partial(near_kernel, group, diag_start),
        grid_spec=pltpu.PrefetchScalarGridSpec(
            num_scalar_prefetch=1, grid=(kv_heads,), in_specs=[q_spec] + [kv_spec] * 4,
            out_specs=[pl.BlockSpec((1, group, HEAD_DIM, rows), lambda g, c: (g, 0, 0, 0)), pl.BlockSpec((1, 2 * group, rows), lambda g, c: (g, 0, 0))],
            scratch_shapes=[pltpu.VMEM((2, block, rows), F32)]),
        out_shape=[jax.ShapeDtypeStruct((kv_heads, group, HEAD_DIM, rows), F32), jax.ShapeDtypeStruct((kv_heads, 2 * group, rows), F32)],
        cost_estimate=pl.CostEstimate(flops=4 * rows * width * block, bytes_accessed=8 * rows * width, transcendentals=rows * width // HEAD_DIM * block),
        compiler_params=pltpu.CompilerParams(dimension_semantics=('arbitrary',)),
        name='near',
    )(counts, q, *other, *own)


def attend_far(counts, q, part, near, far0, far1, after, kv_heads, rows):
    width = q.shape[1]
    group = width // HEAD_DIM // kv_heads
    block = far0[0].shape[0]
    q_spec = pl.BlockSpec((rows, group * HEAD_DIM), lambda g, c: (part, g))
    kv_spec = pl.BlockSpec((block, HEAD_DIM), lambda g, c: (0, g))
    return pl.pallas_call(
        functools.partial(far_kernel, group),
        grid_spec=pltpu.PrefetchScalarGridSpec(
            num_scalar_prefetch=1, grid=(kv_heads,),
            in_specs=[q_spec, pl.BlockSpec((1, group, HEAD_DIM, rows), lambda g, c: (g, 0, 0, 0)), pl.BlockSpec((1, 2 * group, rows), lambda g, c: (g, 0, 0))]
            + [kv_spec] * 4 + [pl.BlockSpec(memory_space=pl.ANY)] * len(after),
            out_specs=pl.BlockSpec((rows, group * HEAD_DIM), lambda g, c: (0, g)),
            scratch_shapes=[pltpu.VMEM((2, block, rows), F32), pltpu.VMEM((group, HEAD_DIM, rows), F32)]),
        out_shape=jax.ShapeDtypeStruct((rows, width), BF16),
        cost_estimate=pl.CostEstimate(flops=8 * rows * width * block, bytes_accessed=8 * rows * width, transcendentals=2 * rows * width // HEAD_DIM * block),
        compiler_params=pltpu.CompilerParams(dimension_semantics=('arbitrary',)),
        name='far',
    )(counts, q, *near, *far0, *far1, *after)


def build_kernel(capacity, n_parts, where, slot_ref, gate_ref, *refs):
    parts, (o_ref, pick_ref, scale_ref) = refs[:n_parts], refs[-3:]
    experts, tokens = slot_ref.shape

    @pl.when(pl.program_id(0) == 0)
    def _():
        rank = lax.broadcasted_iota(jnp.int32, (capacity, tokens), 0)
        for e in range(experts):
            hit = slot_ref[e:e + 1, :] == rank
            pick_ref[e * capacity:(e + 1) * capacity, :] = jnp.where(hit, 1.0, 0.0).astype(BF16)
            picked = jnp.sum(jnp.where(hit, gate_ref[e:e + 1, :], 0.0), axis=1, keepdims=True)
            scale_ref[e * capacity:(e + 1) * capacity, :] = jnp.broadcast_to(picked, (capacity, HEAD_DIM))

    for e in range(experts):
        lo, hi, at = e * capacity, (e + 1) * capacity, 0
        total = None
        for part in parts:
            n = part.shape[0]
            term = jnp.dot(pick_ref[lo:hi, at:at + n], part[...], preferred_element_type=F32)
            total = term if total is None else total + term
            at += n
        o_ref[0, 0, e] = (total * scale_ref[lo:hi, 0:1]).astype(BF16)


def build(where, slots, gates, parts, capacity, prior=None, col=512):
    experts, tokens = slots.shape
    d_model = parts[0].shape[1]
    fixed = pl.BlockSpec((experts, tokens), lambda n, w: (0, 0))
    in_specs = [fixed, fixed] + [pl.BlockSpec((p.shape[0], col), lambda n, w: (0, n)) for p in parts]
    args = [slots, gates, *parts]
    aliases = {}
    if prior is not None:
        in_specs.append(pl.BlockSpec(memory_space=pl.ANY))
        args.append(prior)
        aliases = {len(args): 0}
    return pl.pallas_call(
        functools.partial(build_kernel, capacity, len(parts)),
        grid_spec=pltpu.PrefetchScalarGridSpec(
            num_scalar_prefetch=1, grid=(d_model // col,), in_specs=in_specs,
            out_specs=pl.BlockSpec((1, 1, experts, capacity, col), lambda n, w: (0, w[0], 0, 0, n)),
            scratch_shapes=[pltpu.VMEM((experts * capacity, tokens), BF16), pltpu.VMEM((experts * capacity, HEAD_DIM), F32)]),
        out_shape=jax.ShapeDtypeStruct((1, 2, experts, capacity, d_model), BF16),
        input_output_aliases=aliases,
        cost_estimate=pl.CostEstimate(flops=2 * experts * capacity * tokens * d_model, bytes_accessed=2 * d_model * (tokens + experts * capacity), transcendentals=0),
        compiler_params=pltpu.CompilerParams(dimension_semantics=('arbitrary',)),
        name='build',
    )(where, *args)


def slots_of(ids_rows, experts):
    tok_dev = ids_rows.shape[0]
    routed = jnp.any(ids_rows[:, :, None] == jnp.arange(experts)[None, None, :], axis=1)
    earlier = jnp.arange(tok_dev)[None, :] < jnp.arange(tok_dev)[:, None]
    rank = jnp.dot(earlier.astype(BF16), routed.astype(BF16), preferred_element_type=F32)
    return jnp.where(routed, rank, -1.0).astype(jnp.int32).T


def solution(mesh):
    sp_size = mesh.shape['sp']
    ep_size = mesh.shape['ep']
    pairs = [(i, i ^ 1) for i in range(sp_size)]
    across = [(0, 2), (1, 3)]
    ep_same = [(e * sp_size + s, (1 - e) * sp_size + s) for e in range(ep_size) for s in range(sp_size)]
    ep_cross = [(e * sp_size + s, (1 - e) * sp_size + (s ^ 1)) for e in range(ep_size) for s in range(sp_size)]

    def swap(a):
        return lax.ppermute(a, 'sp', pairs)

    def layer(x_blk, w_query, w_key, w_value, w_out, ids_blk, gate_blk):
        x_own = x_blk[0]
        tok_dev, _ = x_own.shape
        half = tok_dev // 2
        chunk = half // 2
        kv_heads = w_key.shape[1] // HEAD_DIM
        experts = gate_blk.shape[2]
        capacity = capacity_of(tok_dev, ids_blk.shape[2], experts)
        ep = lax.axis_index('ep')
        sp = lax.axis_index('sp')

        x_upper = swap(x_own[half:])
        v_own = jnp.dot(x_own, w_value, preferred_element_type=F32).astype(BF16)
        v_a = lax.ppermute(v_own, 'sp', across)
        k_own = jnp.dot(x_own, w_key, preferred_element_type=F32).astype(BF16)
        k_a = lax.ppermute(k_own, 'sp', across)
        k_mate, v_mate = swap(k_own), swap(v_own)
        v_b = swap(v_a)
        k_b = swap(k_a)
        q_low = jnp.dot(x_own[:half], w_query, preferred_element_type=F32).astype(BF16)
        q_upp = jnp.dot(x_upper, w_query, preferred_element_type=F32).astype(BF16)

        far = (sp >= 2).astype(jnp.int32)
        odd = (sp % 2).astype(jnp.int32)
        counts_low = jnp.stack([odd, far])
        counts_upp = jnp.stack([1 - odd, far])

        ids_other = lax.ppermute(ids_blk[0], ('ep', 'sp'), ep_same)
        gates_other = lax.ppermute(gate_blk[0], ('ep', 'sp'), ep_same)
        local = experts // ep_size

        def mine(a):
            return lax.dynamic_slice_in_dim(a, ep * local, local, 0)

        slots_own, gates_own = mine(slots_of(ids_blk[0], experts)), mine(gate_blk[0].T)
        slots_oth, gates_oth = mine(slots_of(ids_other, experts)), mine(gates_other.T)

        near = []
        for c in range(4):
            lower = c < 2
            near.append(attend_near(counts_low if lower else counts_upp, q_low if lower else q_upp, c % 2, (k_own, v_own) if lower else (k_mate, v_mate),
                                    (k_mate, v_mate) if lower else (k_own, v_own), c * chunk, kv_heads, chunk))
        own_rows, other_rows = [], []
        after = [slots_own, gates_own, slots_oth, gates_oth]
        for c in range(4):
            lower = c < 2
            x_c = lax.slice_in_dim(x_own if lower else x_upper, (c % 2) * chunk, (c % 2 + 1) * chunk, axis=0)
            o_c = attend_far(counts_low if lower else counts_upp, q_low if lower else q_upp, c % 2, near[c], (k_a, v_a), (k_b, v_b), after, kv_heads, chunk)
            mixed = jnp.dot(o_c, w_out, preferred_element_type=F32)
            h_c = (x_c.astype(F32) + mixed).astype(BF16)
            after = [h_c]
            own_rows.append(h_c if lower else swap(h_c))
            other_rows.append(lax.ppermute(h_c, ('ep', 'sp'), ep_same if lower else ep_cross))
        hidden = jnp.concatenate(own_rows, axis=0)
        buf = build(ep[None].astype(jnp.int32), slots_own, gates_own, [hidden], capacity)
        buf = build((1 - ep)[None].astype(jnp.int32), slots_oth, gates_oth, other_rows, capacity, prior=buf)
        return hidden[None], buf

    seq_spec = P(('dp', 'ep'), 'sp', None)
    buf_spec = P(('dp', 'sp'), None, 'ep', None, None)
    return jax.shard_map(layer, mesh=mesh, in_specs=(seq_spec, P(), P(), P(), P(), seq_spec, seq_spec), out_specs=(seq_spec, buf_spec), check_vma=False)
```

time: 748 us -> 610 us (0.82)
  Pallas kernels: 442 us -> 218 us
  waiting for transfers between devices: 61 us -> 206 us
  starting transfers between devices: 73 us -> 18.9 us
    pallas_call x6 -> x10, Pallas kernels: 442 us -> 218 us  [the longest x4 115 us: attend_far(): pl.pallas_call(functools.partial(far_kernel, group), grid_spec=pltpu.Pref...]
    ppermute x8, waiting for transfers between devices: 61 us -> 203 us  [the longest x4 151 us: layer(): lax.ppermute(h_c, ('ep', 'sp'), ep_same if lower else ep_cross)]
    ppermute x8, starting transfers between devices: 70.3 us -> 9.57 us  [the longest x4 4.22 us: layer(): lax.ppermute(h_c, ('ep', 'sp'), ep_same if lower else ep_cross)]
  transfers between devices with their start and end apart: 15 -> 15, of which waited for: 2 -> 9; matrix products, arithmetic and copies ran while one was open for 20% -> 14% of each run, Pallas kernels for 57% -> 19%
where the time goes in v3:
time: 610 us; the launch traced here: 603 us
  Pallas kernels  218 us (36%)
  waiting for transfers between devices  206 us (34%)
  matrix products  142 us (23%)
  starting transfers between devices  18.9 us (3%)
  other arithmetic  11.6 us (2%)
    ppermute x4, waiting for transfers between devices, layer(): lax.ppermute(h_c, ('ep', 'sp'), ep_same if lower else ep_cross)  151 us
    pallas_call x4, Pallas kernels, attend_far(): pl.pallas_call(functools.partial(far_kernel, group), grid_spec=pltpu.Pref...  115 us
    pallas_call x4, Pallas kernels, attend_near(): pl.pallas_call(functools.partial(near_kernel, group, diag_start), grid_sp...  70.9 us
    dot_general x4, matrix products, layer(): mixed = jnp.dot(o_c, w_out, preferred_element_type=F32)  69.5 us
    ppermute x1, waiting for transfers between devices, layer(): k_a = lax.ppermute(k_own, 'sp', across)  42.4 us
    pallas_call x2, Pallas kernels, build(): pl.pallas_call(functools.partial(build_kernel, capacity, len(parts)), gri...  32.2 us
    dot_general x1, matrix products, layer(): q_upp = jnp.dot(x_upper, w_query, preferred_element_type=F32).astype(BF16)  24 us
    dot_general x1, matrix products, layer(): jnp.dot(x_own[:half], w_query, preferred_element_type=F32).astype(BF16)  22.4 us
  transfers between devices with their start and end apart: 15, of which 9 were waited for; matrix products, arithmetic and copies ran while one was open for 14% of the time, Pallas kernels for 19%

profile of v3, /device:TPU:3, one launch (start us, length us, event | category | flops | bytes accessed | tf_op | source)
XLA Modules:
  0.0 603.5 jit_solution(8345502523440667631)
XLA Ops:
  0.7 14.9 %fusion.15.v_own.v_oth = bf16[1024,1024]{1,0:T(8,128)(2,1)} fusion(bf16[4096,1024]{1,0:T(8,128)(2,1)} %param.10, bf16[1,1024,4096]{2,1,0:T(8,128)(2,1)} %param.7), kind=kOutput, calls=%fused_computation.22 | convolution fusion | flops 8590983168 | bytes 18874368 | tf_op jit(solution)/shard_map/dot_general | solution.py:223
  17.7 10.0 %fusion.12.k_own.k_oth = bf16[1024,1024]{1,0:T(8,128)(2,1)} fusion(bf16[4096,1024]{1,0:T(8,128)(2,1)S(1)} %copy-done.4, bf16[1,1024,4096]{2,1,0:T(8,128)(2,1)S(1)} %copy-done.1), kind=kOutput, calls=%fused_computation.21 | convolution fusion | flops 8590983168 | bytes 18874368 | tf_op jit(solution)/shard_map/dot_general | solution.py:225
  27.7 1.5 collective-permute-start.2
  30.5 22.4 %convolution_convert_fusion.1.q_ref = bf16[512,4096]{1,0:T(8,128)(2,1)} fusion(bf16[4096,4096]{1,0:T(8,128)(2,1)} %param.8, bf16[1,1024,4096]{2,1,0:T(8,128)(2,1)S(1)} %copy-done.1), kind=kOutput, calls=%fused_computation.6 | convolution fusion | flops 17181966336 | bytes 41943040 | tf_op jit(solution)/shard_map/dot_general | solution.py:230
  55.1 9.1 %collective-permute-done.3.va = bf16[1024,1024]{1,0:T(8,128)(2,1)S(1)} collective-permute-done((bf16[1024,1024]{1,0:T(8,128)(2,1)}, bf16[1024,1024]{1,0:T(8,128)(2,1)S(1)}, u32[]{:S(2)}, u32[]{:S(2)}) %collective-permute-start.3) | collective-permute-done | bytes 2097184 | tf_op jit(solution)/shard_map/ppermute | solution.py:224
  64.3 2.7 collective-permute-start.5
  66.9 42.4 %collective-permute-done.2.ka = bf16[1024,1024]{1,0:T(8,128)(2,1)} collective-permute-done((bf16[1024,1024]{1,0:T(8,128)(2,1)}, bf16[1024,1024]{1,0:T(8,128)(2,1)}, u32[]{:S(2)}, u32[]{:S(2)}) %collective-permute-start.2) | collective-permute-done | bytes 2097184 | tf_op jit(solution)/shard_map/ppermute | solution.py:226
  109.3 1.5 collective-permute-start.4
  110.8 4.7 slice_bitcast_fusion
  121.3 21.8 %near.5 = (f32[8,4,128,256]{3,2,1,0:T(8,128)}, f32[8,8,256]{2,1,0:T(8,128)}) custom-call(s32[2]{0:T(128)} %pad_add_fusion.counts, bf16[512,4096]{1,0:T(8,128)(2,1)} %convolution_convert_fusion.1.q_ref, bf16[1024,1024]{1,0:T(8,128)(2,1)} %collective-permute-done.k_oth.k_own, bf16[1024,1024]{1,0:T(8,128)(2,1)} %collective-permute-done.1.v_oth.v_own, ...), custom_call_target="tpu_custom_call" | custom-call | flops 4294967296 | bytes 8388608 | tf_op jit(solution)/shard_map/near/pallas_call | solution.py:109
  143.2 20.6 %near.4 = (f32[8,4,128,256]{3,2,1,0:T(8,128)}, f32[8,8,256]{2,1,0:T(8,128)}) custom-call(s32[2]{0:T(128)} %pad_add_fusion.counts, bf16[512,4096]{1,0:T(8,128)(2,1)} %convolution_convert_fusion.1.q_ref, bf16[1024,1024]{1,0:T(8,128)(2,1)} %collective-permute-done.k_oth.k_own, bf16[1024,1024]{1,0:T(8,128)(2,1)} %collective-permute-done.1.v_oth.v_own, ...), custom_call_target="tpu_custom_call" | custom-call | flops 4294967296 | bytes 8388608 | tf_op jit(solution)/shard_map/near/pallas_call | solution.py:109
  163.8 28.8 %far.4 = bf16[256,4096]{1,0:T(8,128)(2,1)} custom-call(s32[2]{0:T(128)} %pad_add_fusion.counts, bf16[512,4096]{1,0:T(8,128)(2,1)} %convolution_convert_fusion.1.q_ref, f32[8,4,128,256]{3,2,1,0:T(8,128)} %get-tuple-element.10.acc_in, f32[8,8,256]{2,1,0:T(8,128)} %get-tuple-element.11.ml_ref, bf16[1024,1024]{1,0:T(8,128)(2,1)} %collective-permute-done.2.ka, ...), custom_call_target="tpu_custom_call" | custom-call | flops 8589934592 | bytes 8388608 | tf_op jit(solution)/shard_map/far/pallas_call | solution.py:128
  192.6 17.4 %fusion.4.refs_0_ = bf16[256,4096]{1,0:T(8,128)(2,1)} fusion(bf16[256,4096]{1,0:T(8,128)(2,1)} %far.4, bf16[4096,4096]{1,0:T(8,128)(2,1)} %param.11, bf16[1,1024,4096]{2,1,0:T(8,128)(2,1)} %param.7), kind=kOutput, calls=%fused_computation.11 | convolution fusion | flops 8593080320 | bytes 39845888 | tf_op jit(solution)/shard_map/dot_general | solution.py:259
  210.0 28.7 %far.5 = bf16[256,4096]{1,0:T(8,128)(2,1)} custom-call(s32[2]{0:T(128)} %pad_add_fusion.counts, bf16[512,4096]{1,0:T(8,128)(2,1)} %convolution_convert_fusion.1.q_ref, f32[8,4,128,256]{3,2,1,0:T(8,128)} %get-tuple-element.12.acc_in, f32[8,8,256]{2,1,0:T(8,128)} %get-tuple-element.13.ml_ref, bf16[1024,1024]{1,0:T(8,128)(2,1)} %collective-permute-done.2.ka, ...), custom_call_target="tpu_custom_call" | custom-call | flops 8589934592 | bytes 8388608 | tf_op jit(solution)/shard_map/far/pallas_call | solution.py:128
  238.7 17.3 %fusion.5.refs_0_ = bf16[256,4096]{1,0:T(8,128)(2,1)} fusion(bf16[256,4096]{1,0:T(8,128)(2,1)} %far.5, bf16[4096,4096]{1,0:T(8,128)(2,1)} %param.11, bf16[1,1024,4096]{2,1,0:T(8,128)(2,1)} %param.7), kind=kOutput, calls=%fused_computation.12 | convolution fusion | flops 8593080320 | bytes 39845888 | tf_op jit(solution)/shard_map/dot_general | solution.py:259
  256.0 24.0 %convolution_convert_fusion.q_ref = bf16[512,4096]{1,0:T(8,128)(2,1)} fusion(bf16[512,4096]{1,0:T(8,128)(2,1)} %collective-permute-done.8, bf16[4096,4096]{1,0:T(8,128)(2,1)} %param.8), kind=kOutput, calls=%fused_computation.5 | convolution fusion | flops 17181966336 | bytes 41943040 | tf_op jit(solution)/shard_map/dot_general | solution.py:231
  280.0 14.5 %near.7 = (f32[8,4,128,256]{3,2,1,0:T(8,128)}, f32[8,8,256]{2,1,0:T(8,128)}) custom-call(s32[2]{0:T(128)} %pad_add_fusion.1.counts, bf16[512,4096]{1,0:T(8,128)(2,1)} %convolution_convert_fusion.q_ref, bf16[1024,1024]{1,0:T(8,128)(2,1)} %fusion.12.k_own.k_oth, bf16[1024,1024]{1,0:T(8,128)(2,1)} %fusion.15.v_own.v_oth, ...), custom_call_target="tpu_custom_call" | custom-call | flops 4294967296 | bytes 8388608 | tf_op jit(solution)/shard_map/near/pallas_call | solution.py:109
  294.5 14.0 %near.6 = (f32[8,4,128,256]{3,2,1,0:T(8,128)}, f32[8,8,256]{2,1,0:T(8,128)}) custom-call(s32[2]{0:T(128)} %pad_add_fusion.1.counts, bf16[512,4096]{1,0:T(8,128)(2,1)} %convolution_convert_fusion.q_ref, bf16[1024,1024]{1,0:T(8,128)(2,1)} %fusion.12.k_own.k_oth, bf16[1024,1024]{1,0:T(8,128)(2,1)} %fusion.15.v_own.v_oth, ...), custom_call_target="tpu_custom_call" | custom-call | flops 4294967296 | bytes 8388608 | tf_op jit(solution)/shard_map/near/pallas_call | solution.py:109
  308.5 28.8 %far.6 = bf16[256,4096]{1,0:T(8,128)(2,1)} custom-call(s32[2]{0:T(128)} %pad_add_fusion.1.counts, bf16[512,4096]{1,0:T(8,128)(2,1)} %convolution_convert_fusion.q_ref, f32[8,4,128,256]{3,2,1,0:T(8,128)} %get-tuple-element.14.acc_in, f32[8,8,256]{2,1,0:T(8,128)} %get-tuple-element.15.ml_ref, bf16[1024,1024]{1,0:T(8,128)(2,1)} %collective-permute-done.2.ka, ...), custom_call_target="tpu_custom_call" | custom-call | flops 8589934592 | bytes 8388608 | tf_op jit(solution)/shard_map/far/pallas_call | solution.py:128
  337.3 17.4 %fusion.6.refs_0_ = bf16[256,4096]{1,0:T(8,128)(2,1)} fusion(bf16[256,4096]{1,0:T(8,128)(2,1)} %far.6, bf16[4096,4096]{1,0:T(8,128)(2,1)} %param.11, bf16[512,4096]{1,0:T(8,128)(2,1)} %collective-permute-done.8), kind=kOutput, calls=%fused_computation.13 | convolution fusion | flops 8593080320 | bytes 39845888 | tf_op jit(solution)/shard_map/dot_general | solution.py:259
  354.7 28.7 %far.7 = bf16[256,4096]{1,0:T(8,128)(2,1)} custom-call(s32[2]{0:T(128)} %pad_add_fusion.1.counts, bf16[512,4096]{1,0:T(8,128)(2,1)} %convolution_convert_fusion.q_ref, f32[8,4,128,256]{3,2,1,0:T(8,128)} %get-tuple-element.16.acc_in, f32[8,8,256]{2,1,0:T(8,128)} %get-tuple-element.17.ml_ref, bf16[1024,1024]{1,0:T(8,128)(2,1)} %collective-permute-done.2.ka, ...), custom_call_target="tpu_custom_call" | custom-call | flops 8589934592 | bytes 8388608 | tf_op jit(solution)/shard_map/far/pallas_call | solution.py:128
  383.5 17.4 %fusion.7 = bf16[256,4096]{1,0:T(8,128)(2,1)} fusion(bf16[256,4096]{1,0:T(8,128)(2,1)} %far.7, bf16[4096,4096]{1,0:T(8,128)(2,1)} %param.11, bf16[512,4096]{1,0:T(8,128)(2,1)} %collective-permute-done.8), kind=kOutput, calls=%fused_computation.14 | convolution fusion | flops 8593080320 | bytes 39845888 | tf_op jit(solution)/shard_map/dot_general | solution.py:259
  400.8 3.5 collective-permute-start.10
  404.3 1.6 collective-permute-start.14
  409.7 1.8 collective-permute-done.9
  411.4 9.1 %pad_maximum_fusion = (bf16[1024,4096]{1,0:T(8,128)(2,1)}, bf16[1,1024,4096]{2,1,0:T(8,128)(2,1)}) fusion(bf16[256,4096]{1,0:T(8,128)(2,1)} %collective-permute-done.10, bf16[256,4096]{1,0:T(8,128)(2,1)} %collective-permute-done.9, bf16[256,4096]{1,0:T(8,128)(2,1)} %fusion.5.refs_0_, bf16[256,4096]{1,0:T(8,128)(2,1)S(1)} %copy-done), kind=kLoop, calls=%fused_computation | loop fusion | flops 33554432 | bytes 25165824 | tf_op jit(solution)/shard_map/concatenate | solution.py:264
  420.5 16.3 %build.2.refs_4_ = bf16[1,2,8,160,4096]{4,3,2,1,0:T(8,128)(2,1)} custom-call(s32[1]{0:T(128)} %bitcast.17.where, s32[8,1024]{1,0:T(8,128)} %fusion.23.refs_0_.slot_ref, f32[8,1024]{1,0:T(8,128)} %dynamic-slice_bitcast_fusion.1.refs_1_.gate_ref, bf16[1024,4096]{1,0:T(8,128)(2,1)} %get-tuple-element.18.refs_0_), custom_call_target="tpu_custom_call" | custom-call | flops 10737418240 | bytes 18874368 | tf_op jit(solution)/shard_map/build/pallas_call | solution.py:178
  436.8 16.1 %collective-permute-done.14.refs_3_ = bf16[256,4096]{1,0:T(8,128)(2,1)} collective-permute-done((bf16[256,4096]{1,0:T(8,128)(2,1)}, bf16[256,4096]{1,0:T(8,128)(2,1)}, u32[]{:S(2)}, u32[]{:S(2)}) %collective-permute-start.14) | collective-permute-done | bytes 2097184 | tf_op jit(solution)/shard_map/ppermute | solution.py:263
  452.9 44.6 %collective-permute-done.13.refs_2_ = bf16[256,4096]{1,0:T(8,128)(2,1)} collective-permute-done((bf16[256,4096]{1,0:T(8,128)(2,1)}, bf16[256,4096]{1,0:T(8,128)(2,1)}, u32[]{:S(2)}, u32[]{:S(2)}) %collective-permute-start.13) | collective-permute-done | bytes 2097184 | tf_op jit(solution)/shard_map/ppermute | solution.py:263
  497.5 44.9 %collective-permute-done.12.refs_1_ = bf16[256,4096]{1,0:T(8,128)(2,1)} collective-permute-done((bf16[256,4096]{1,0:T(8,128)(2,1)}, bf16[256,4096]{1,0:T(8,128)(2,1)}, u32[]{:S(2)}, u32[]{:S(2)}) %collective-permute-start.12) | collective-permute-done | bytes 2097184 | tf_op jit(solution)/shard_map/ppermute | solution.py:263
  542.4 44.9 %collective-permute-done.11.refs_0_ = bf16[256,4096]{1,0:T(8,128)(2,1)} collective-permute-done((bf16[256,4096]{1,0:T(8,128)(2,1)S(1)}, bf16[256,4096]{1,0:T(8,128)(2,1)}, u32[]{:S(2)}, u32[]{:S(2)}) %collective-permute-start.11) | collective-permute-done | bytes 2097184 | tf_op jit(solution)/shard_map/ppermute | solution.py:263
  587.3 15.9 %build.3 = bf16[1,2,8,160,4096]{4,3,2,1,0:T(8,128)(2,1)} custom-call(s32[1]{0:T(128)} %bitcast.16.where, s32[8,1024]{1,0:T(8,128)} %fusion.21.refs_2_.slot_ref, f32[8,1024]{1,0:T(8,128)} %dynamic-slice_bitcast_fusion.refs_3_.gate_ref, bf16[256,4096]{1,0:T(8,128)(2,1)} %collective-permute-done.11.refs_0_, ...), custom_call_target="tpu_custom_call", output_to_operand_aliasing={{}: (7, {})} | custom-call | flops 10737418240 | bytes 18874368 | tf_op jit(solution)/shard_map/build/pallas_call | solution.py:178
  (40 shorter events, 15.3 us)
Async XLA Ops:
  0.6 17.0 %copy-start.1 = (bf16[1,1024,4096]{2,1,0:T(8,128)(2,1)S(1)}, bf16[1,1024,4096]{2,1,0:T(8,128)(2,1)}, u32[]{:S(2)}) copy-start(bf16[1,1024,4096]{2,1,0:T(8,128)(2,1)} %param.7) | copy-start | bytes 25165828
  0.6 17.0 %copy-start.4 = (bf16[4096,1024]{1,0:T(8,128)(2,1)S(1)}, bf16[4096,1024]{1,0:T(8,128)(2,1)}, u32[]{:S(2)}) copy-start(bf16[4096,1024]{1,0:T(8,128)(2,1)} %param.9) | copy-start | bytes 25165828
  15.5 13.7 %copy-start.3 = (s32[1,1024,2]{1,2,0:T(2,128)S(1)}, s32[1,1024,2]{1,2,0:T(2,128)}, u32[]{:S(2)}) copy-start(s32[1,1024,2]{1,2,0:T(2,128)} %param.12) | copy-start | bytes 24580
  15.5 48.7 %collective-permute-start.3 = (bf16[1024,1024]{1,0:T(8,128)(2,1)}, bf16[1024,1024]{1,0:T(8,128)(2,1)S(1)}, u32[]{:S(2)}, u32[]{:S(2)}) collective-permute-start(bf16[1024,1024]{1,0:T(8,128)(2,1)} %fusion.15.v_own.v_oth), channel_id=1, source_target_pairs={{0,2},{1,3},{4,6},{5,7}} | collective-permute-start | bytes 6291464 | tf_op jit(solution)/shard_map/ppermute | solution.py:224
  17.0 104.4 %collective-permute-start.1 = (bf16[1024,1024]{1,0:T(8,128)(2,1)}, bf16[1024,1024]{1,0:T(8,128)(2,1)}, u32[]{:S(2)}, u32[]{:S(2)}) collective-permute-start(bf16[1024,1024]{1,0:T(8,128)(2,1)} %fusion.15.v_own.v_oth), channel_id=1, source_target_pairs={{0,1},{1,0},{2,3},{3,2},{4,5},{5,4},{6,7},{7,6}} | collective-permute-start | bytes 6291464 | tf_op jit(solution)/shard_map/ppermute | solution.py:209
  27.7 81.6 %collective-permute-start.2 = (bf16[1024,1024]{1,0:T(8,128)(2,1)}, bf16[1024,1024]{1,0:T(8,128)(2,1)}, u32[]{:S(2)}, u32[]{:S(2)}) collective-permute-start(bf16[1024,1024]{1,0:T(8,128)(2,1)} %fusion.12.k_own.k_oth), channel_id=1, source_target_pairs={{0,2},{1,3},{4,6},{5,7}} | collective-permute-start | bytes 6291464 | tf_op jit(solution)/shard_map/ppermute | solution.py:226
  29.1 92.2 %collective-permute-start = (bf16[1024,1024]{1,0:T(8,128)(2,1)}, bf16[1024,1024]{1,0:T(8,128)(2,1)}, u32[]{:S(2)}, u32[]{:S(2)}) collective-permute-start(bf16[1024,1024]{1,0:T(8,128)(2,1)} %fusion.12.k_own.k_oth), channel_id=1, source_target_pairs={{0,1},{1,0},{2,3},{3,2},{4,5},{5,4},{6,7},{7,6}} | collective-permute-start | bytes 6291464 | tf_op jit(solution)/shard_map/ppermute | solution.py:209
  29.2 24.2 %copy-start.2 = (f32[1,1024,16]{1,2,0:T(8,128)S(1)}, f32[1,1024,16]{1,2,0:T(8,128)}, u32[]{:S(2)}) copy-start(f32[1,1024,16]{1,2,0:T(8,128)} %param.13) | copy-start | bytes 196612
  29.2 87.0 %collective-permute-start.6 = (s32[1024,2]{0,1:T(2,128)S(1)}, s32[1024,2]{0,1:T(2,128)S(1)}, u32[]{:S(2)}, u32[]{:S(2)}) collective-permute-start(s32[1024,2]{0,1:T(2,128)S(1)} %bitcast.55), channel_id=1, source_target_pairs={{0,4},{1,5},{2,6},{3,7},{4,0},{5,1},{6,2},{7,3}} | collective-permute-start | bytes 24584 | tf_op jit(solution)/shard_map/ppermute | solution.py:238
  64.3 51.3 %copy-start.5 = (bf16[1024,1024]{1,0:T(8,128)(2,1)}, bf16[1024,1024]{1,0:T(8,128)(2,1)S(1)}, u32[]{:S(2)}) copy-start(bf16[1024,1024]{1,0:T(8,128)(2,1)S(1)} %collective-permute-done.3.va) | copy-start | bytes 6291460
  64.3 99.5 %collective-permute-start.5 = (bf16[1024,1024]{1,0:T(8,128)(2,1)S(1)}, bf16[1024,1024]{1,0:T(8,128)(2,1)}, u32[]{:S(2)}, u32[]{:S(2)}) collective-permute-start(bf16[1024,1024]{1,0:T(8,128)(2,1)S(1)} %collective-permute-done.3.va), channel_id=1, source_target_pairs={{0,1},{1,0},{2,3},{3,2},{4,5},{5,4},{6,7},{7,6}} | collective-permute-start | bytes 6291464 | tf_op jit(solution)/shard_map/ppermute | solution.py:209
  109.3 54.5 %collective-permute-start.4 = (bf16[1024,1024]{1,0:T(8,128)(2,1)}, bf16[1024,1024]{1,0:T(8,128)(2,1)}, u32[]{:S(2)}, u32[]{:S(2)}) collective-permute-start(bf16[1024,1024]{1,0:T(8,128)(2,1)} %collective-permute-done.2.ka), channel_id=1, source_target_pairs={{0,1},{1,0},{2,3},{3,2},{4,5},{5,4},{6,7},{7,6}} | collective-permute-start | bytes 6291464 | tf_op jit(solution)/shard_map/ppermute | solution.py:209
  116.2 3.6 collective-permute-start.7
  119.9 136.2 %collective-permute-start.8 = (bf16[512,4096]{1,0:T(8,128)(2,1)}, bf16[512,4096]{1,0:T(8,128)(2,1)}, u32[]{:S(2)}, u32[]{:S(2)}) collective-permute-start(bf16[512,4096]{1,0:T(8,128)(2,1)} %slice_bitcast_fusion), channel_id=1, source_target_pairs={{0,1},{1,0},{2,3},{3,2},{4,5},{5,4},{6,7},{7,6}} | collective-permute-start | bytes 12582920 | tf_op jit(solution)/shard_map/ppermute | solution.py:209
  383.5 25.0 %copy-start = (bf16[256,4096]{1,0:T(8,128)(2,1)S(1)}, bf16[256,4096]{1,0:T(8,128)(2,1)}, u32[]{:S(2)}) copy-start(bf16[256,4096]{1,0:T(8,128)(2,1)} %fusion.4.refs_0_) | copy-start | bytes 6291460
  400.8 7.6 %collective-permute-start.10 = (bf16[256,4096]{1,0:T(8,128)(2,1)}, bf16[256,4096]{1,0:T(8,128)(2,1)}, u32[]{:S(2)}, u32[]{:S(2)}) collective-permute-start(bf16[256,4096]{1,0:T(8,128)(2,1)} %fusion.7), channel_id=1, source_target_pairs={{0,1},{1,0},{2,3},{3,2},{4,5},{5,4},{6,7},{7,6}} | collective-permute-start | bytes 6291464 | tf_op jit(solution)/shard_map/ppermute | solution.py:209
  404.3 7.1 %collective-permute-start.9 = (bf16[256,4096]{1,0:T(8,128)(2,1)}, bf16[256,4096]{1,0:T(8,128)(2,1)}, u32[]{:S(2)}, u32[]{:S(2)}) collective-permute-start(bf16[256,4096]{1,0:T(8,128)(2,1)} %fusion.6.refs_0_), channel_id=1, source_target_pairs={{0,1},{1,0},{2,3},{3,2},{4,5},{5,4},{6,7},{7,6}} | collective-permute-start | bytes 6291464 | tf_op jit(solution)/shard_map/ppermute | solution.py:209
  404.3 48.5 %collective-permute-start.14 = (bf16[256,4096]{1,0:T(8,128)(2,1)}, bf16[256,4096]{1,0:T(8,128)(2,1)}, u32[]{:S(2)}, u32[]{:S(2)}) collective-permute-start(bf16[256,4096]{1,0:T(8,128)(2,1)} %fusion.7), channel_id=1, source_target_pairs={{0,5},{1,4},{2,7},{3,6},{4,1},{5,0},{6,3},{7,2}} | collective-permute-start | bytes 6291464 | tf_op jit(solution)/shard_map/ppermute | solution.py:263
  406.0 91.6 %collective-permute-start.13 = (bf16[256,4096]{1,0:T(8,128)(2,1)}, bf16[256,4096]{1,0:T(8,128)(2,1)}, u32[]{:S(2)}, u32[]{:S(2)}) collective-permute-start(bf16[256,4096]{1,0:T(8,128)(2,1)} %fusion.6.refs_0_), channel_id=1, source_target_pairs={{0,5},{1,4},{2,7},{3,6},{4,1},{5,0},{6,3},{7,2}} | collective-permute-start | bytes 6291464 | tf_op jit(solution)/shard_map/ppermute | solution.py:263
  406.1 136.3 %collective-permute-start.12 = (bf16[256,4096]{1,0:T(8,128)(2,1)}, bf16[256,4096]{1,0:T(8,128)(2,1)}, u32[]{:S(2)}, u32[]{:S(2)}) collective-permute-start(bf16[256,4096]{1,0:T(8,128)(2,1)} %fusion.5.refs_0_), channel_id=1, source_target_pairs={{0,4},{1,5},{2,6},{3,7},{4,0},{5,1},{6,2},{7,3}} | collective-permute-start | bytes 6291464 | tf_op jit(solution)/shard_map/ppermute | solution.py:263
  408.5 178.9 %collective-permute-start.11 = (bf16[256,4096]{1,0:T(8,128)(2,1)S(1)}, bf16[256,4096]{1,0:T(8,128)(2,1)}, u32[]{:S(2)}, u32[]{:S(2)}) collective-permute-start(bf16[256,4096]{1,0:T(8,128)(2,1)S(1)} %copy-done), channel_id=1, source_target_pairs={{0,4},{1,5},{2,6},{3,7},{4,0},{5,1},{6,2},{7,3}} | collective-permute-start | bytes 6291464 | tf_op jit(solution)/shard_map/ppermute | solution.py:263
